TPU v7x, 32 devices: a whole 2x2x4 slice. The times are simulated.
32 devices in a mesh: data: 2 (over x), dap2: 4 (over z), dap: 4 (over y, core).
Axes of the slice: x: 2, y: 2, z: 4, core: 2. Of those that a mesh axis runs over, the one named last changes fastest.
Arguments:
- pair_act: bfloat16 [1280, 640, 128], P(('data', 'dap'), 'dap2'), parts along dimension 0
- pair_mask: int32 [1280, 640], P(('data', 'dap'), 'dap2'), parts along dimension 0
- in_gamma: float32 [2, 2, 128], replicated
- in_beta: float32 [2, 2, 128], replicated
- w_proj: bfloat16 [2, 2, 128, 512], replicated
- w_gate: bfloat16 [2, 2, 128, 128], replicated
- out_gamma: float32 [2, 2, 128], replicated
- out_beta: float32 [2, 2, 128], replicated
- w_out: bfloat16 [2, 2, 128, 128], replicated
Outputs:
- output: bfloat16 [1280, 640, 128], P(('data', 'dap'), 'dap2'), parts along dimension 0
There are 2 independent parts. A program takes and returns all parts, laid end to end along the dimension named above; an argument that names none is the same for every part.
All inputs are finite; a program needn't handle non-finite values.
Results may differ from a plain program's by a relative error of at most 0.0112834.
Values are sent between devices in bfloat16 or wider.
A program may use at most 1 GiB of HBM per device.

v0:
```python
import jax
import jax.numpy as jnp
from jax import lax
from jax.sharding import PartitionSpec as P

NORM_EPS = 1e-5
OUT_FORM = 'cik,cjk->cij'
IN_FORM = 'cki,ckj->cij'


def layer_norm(values, gamma, beta, axis):
    centered = values - jnp.mean(values, axis=axis, keepdims=True)
    variance = jnp.mean(centered * centered, axis=axis, keepdims=True)
    return centered * lax.rsqrt(variance + NORM_EPS) * gamma + beta


def project_local(pair_blk, mask_f, gamma_in, beta_in, w_proj, w_gate):
    tri_dim = w_proj.shape[1] // 4
    normed = layer_norm(pair_blk.astype(jnp.float32), gamma_in, beta_in, -1).astype(jnp.bfloat16)
    projected = jnp.einsum('ijd,dgc->gcij', normed, w_proj.reshape(w_proj.shape[0], 4, tri_dim), preferred_element_type=jnp.float32)
    left = (mask_f * jax.nn.sigmoid(projected[1]) * projected[0]).astype(jnp.bfloat16)
    right = (mask_f * jax.nn.sigmoid(projected[3]) * projected[2]).astype(jnp.bfloat16)
    gate = jax.nn.sigmoid(jnp.einsum('ijd,de->ije', normed, w_gate, preferred_element_type=jnp.float32))
    return left, right, gate


def finish_local(pair_blk, tri_blk, gate, gamma_out, beta_out, w_out):
    tri_normed = layer_norm(tri_blk.astype(jnp.float32), gamma_out[:, None, None], beta_out[:, None, None], 0).astype(jnp.bfloat16)
    update = jnp.einsum('cij,cd->ijd', tri_normed, w_out, preferred_element_type=jnp.float32)
    return (pair_blk.astype(jnp.float32) + gate * update).astype(jnp.bfloat16)


def to_channels(block):
    col_full = lax.all_to_all(block, 'dap2', 0, 2, tiled=True)
    return lax.all_to_all(col_full, 'dap', 0, 1, tiled=True)


def from_channels(block):
    row_part = lax.all_to_all(block, 'dap', 1, 0, tiled=True)
    return lax.all_to_all(row_part, 'dap2', 2, 0, tiled=True)


def triangle_update(pair_blk, mask_f, params, einsum_form):
    gamma_in, beta_in, w_proj, w_gate, gamma_out, beta_out, w_out = params
    left, right, gate = project_local(pair_blk, mask_f, gamma_in, beta_in, w_proj, w_gate)
    left_ch = to_channels(left)
    right_ch = to_channels(right)
    tri_ch = jnp.einsum(einsum_form, left_ch, right_ch, preferred_element_type=jnp.float32).astype(jnp.bfloat16)
    return finish_local(pair_blk, from_channels(tri_ch), gate, gamma_out, beta_out, w_out)


def solution(mesh):
    pair_spec = P(('data', 'dap'), 'dap2', None)
    mask_spec = P(('data', 'dap'), 'dap2')
    weight_spec = P()

    def local_fn(pair_act, pair_mask, in_gamma, in_beta, w_proj, w_gate, out_gamma, out_beta, w_out):
        mask_f = pair_mask.astype(jnp.float32)
        weights = (in_gamma, in_beta, w_proj, w_gate, out_gamma, out_beta, w_out)
        for layer in range(in_gamma.shape[0]):
            for direction, einsum_form in enumerate((OUT_FORM, IN_FORM)):
                params = tuple(leaf[layer, direction] for leaf in weights)
                pair_act = triangle_update(pair_act, mask_f, params, einsum_form)
        return pair_act

    return jax.shard_map(local_fn, mesh=mesh, in_specs=(pair_spec, mask_spec) + (weight_spec,) * 7, out_specs=pair_spec, check_vma=False)
```

profile of v0, /device:TPU:0, one launch (start us, length us, event | category | flops | bytes accessed | tf_op | source)
XLA Modules:
  0.0 4604.1 jit_solution(5957050717366689356)
XLA Ops:
  20.1 17.7 convolution_bitcast_fusion.3
  37.7 23.0 fusion.71
  60.7 15.1 copy.224
  97.2 213.9 %all-to-all-done = bf16[128,160,160]{2,1,0:T(8,128)(2,1)} async-done(((bf16[128,160,160]{2,1,0:T(8,128)(2,1)}), bf16[128,160,160]{2,1,0:T(8,128)(2,1)}, u32[]{:S(2)}, u32[]{:S(2)}) %all-to-all-start) | async-done | bytes 6553632 | tf_op jit(solution)/shard_map/all_to_all | solution.py:34
  330.6 15.2 all_to_all.291
  345.8 198.6 %all-to-all-done.2 = bf16[128,160,160]{2,1,0:T(8,128)(2,1)} async-done(((bf16[128,160,160]{2,1,0:T(8,128)(2,1)}), bf16[128,160,160]{2,1,0:T(8,128)(2,1)}, u32[]{:S(2)}, u32[]{:S(2)}) %all-to-all-start.2) | async-done | bytes 6553632 | tf_op jit(solution)/shard_map/all_to_all | solution.py:34
  563.2 15.2 all_to_all.299
  578.5 44.4 all-to-all-done.1
  634.9 66.7 %all-to-all-done.3 = bf16[32,160,640]{2,1,0:T(8,128)(2,1)} async-done(((bf16[32,160,640]{2,1,0:T(8,128)(2,1)}), bf16[32,160,640]{2,1,0:T(8,128)(2,1)}, u32[]{:S(2)}, u32[]{:S(2)}) %all-to-all-start.3) | async-done | bytes 6553632 | tf_op jit(solution)/shard_map/all_to_all | solution.py:35
  720.3 76.1 %all_to_all.396 = bf16[8,640,640]{2,0,1:T(8,128)(2,1)S(1)} all-to-all(bf16[8,640,640]{2,0,1:T(8,128)(2,1)S(1)} %copy.231), channel_id=1, replica_groups=mesh['data'=2,'dap2'=4,'dap'=4] {'dap'}, dimensions={1} | all-to-all | bytes 13107200 | tf_op jit(solution)/shard_map/all_to_all | solution.py:39
  800.1 16.0 copy.234
  837.4 212.4 %all-to-all-done.5 = bf16[32,160,640]{1,0,2:T(8,128)(2,1)} async-done(((bf16[32,160,640]{1,0,2:T(8,128)(2,1)}), bf16[32,160,640]{1,0,2:T(8,128)(2,1)}, u32[]{:S(2)}, u32[]{:S(2)}) %all-to-all-start.5) | async-done | bytes 6553632 | tf_op jit(solution)/shard_map/all_to_all | solution.py:40
  1049.8 15.3 copy.235
  1065.0 19.8 reshape.181
  1104.5 17.7 add_convert_fusion.3
  1122.1 19.8 copy.324
  1142.0 18.7 convert_reduce_fusion.2
  1172.0 20.4 convolution_bitcast_fusion.2
  1192.4 22.9 fusion.57
  1215.3 15.1 copy.243
  1251.4 212.2 %all-to-all-done.6 = bf16[128,160,160]{2,1,0:T(8,128)(2,1)} async-done(((bf16[128,160,160]{2,1,0:T(8,128)(2,1)}), bf16[128,160,160]{2,1,0:T(8,128)(2,1)}, u32[]{:S(2)}, u32[]{:S(2)}) %all-to-all-start.6) | async-done | bytes 6553632 | tf_op jit(solution)/shard_map/all_to_all | solution.py:34
  1483.1 15.2 all_to_all.312
  1498.3 198.5 %all-to-all-done.8 = bf16[128,160,160]{2,1,0:T(8,128)(2,1)} async-done(((bf16[128,160,160]{2,1,0:T(8,128)(2,1)}), bf16[128,160,160]{2,1,0:T(8,128)(2,1)}, u32[]{:S(2)}, u32[]{:S(2)}) %all-to-all-start.8) | async-done | bytes 6553632 | tf_op jit(solution)/shard_map/all_to_all | solution.py:34
  1715.7 15.3 all_to_all.320
  1730.9 44.4 all-to-all-done.7
  1787.2 66.8 %all-to-all-done.9 = bf16[32,160,640]{2,1,0:T(8,128)(2,1)} async-done(((bf16[32,160,640]{2,1,0:T(8,128)(2,1)}), bf16[32,160,640]{2,1,0:T(8,128)(2,1)}, u32[]{:S(2)}, u32[]{:S(2)}) %all-to-all-start.9) | async-done | bytes 6553632 | tf_op jit(solution)/shard_map/all_to_all | solution.py:35
  1880.5 76.5 %all_to_all.397 = bf16[8,640,640]{2,0,1:T(8,128)(2,1)S(1)} all-to-all(bf16[8,640,640]{2,0,1:T(8,128)(2,1)S(1)} %copy.250), channel_id=1, replica_groups=mesh['data'=2,'dap2'=4,'dap'=4] {'dap'}, dimensions={1} | all-to-all | bytes 13107200 | tf_op jit(solution)/shard_map/all_to_all | solution.py:39
  1960.6 16.0 copy.253
  1997.2 213.0 %all-to-all-done.11 = bf16[32,160,640]{1,0,2:T(8,128)(2,1)} async-done(((bf16[32,160,640]{1,0,2:T(8,128)(2,1)}), bf16[32,160,640]{1,0,2:T(8,128)(2,1)}, u32[]{:S(2)}, u32[]{:S(2)}) %all-to-all-start.11) | async-done | bytes 6553632 | tf_op jit(solution)/shard_map/all_to_all | solution.py:40
  2210.3 15.4 copy.254
  2225.6 19.8 reshape.182
  2274.3 19.6 copy.325
  2293.9 18.6 convert_reduce_fusion.1
  2323.8 20.4 convolution_bitcast_fusion.1
  2344.2 22.9 fusion.43
  2367.1 15.1 copy.262
  2403.2 212.2 %all-to-all-done.12 = bf16[128,160,160]{2,1,0:T(8,128)(2,1)} async-done(((bf16[128,160,160]{2,1,0:T(8,128)(2,1)}), bf16[128,160,160]{2,1,0:T(8,128)(2,1)}, u32[]{:S(2)}, u32[]{:S(2)}) %all-to-all-start.12) | async-done | bytes 6553632 | tf_op jit(solution)/shard_map/all_to_all | solution.py:34
  2635.3 15.2 all_to_all.333
  2650.5 198.5 %all-to-all-done.14 = bf16[128,160,160]{2,1,0:T(8,128)(2,1)} async-done(((bf16[128,160,160]{2,1,0:T(8,128)(2,1)}), bf16[128,160,160]{2,1,0:T(8,128)(2,1)}, u32[]{:S(2)}, u32[]{:S(2)}) %all-to-all-start.14) | async-done | bytes 6553632 | tf_op jit(solution)/shard_map/all_to_all | solution.py:34
  2867.9 15.2 all_to_all.341
  2883.1 44.4 all-to-all-done.13
  2939.2 66.8 %all-to-all-done.15 = bf16[32,160,640]{2,1,0:T(8,128)(2,1)} async-done(((bf16[32,160,640]{2,1,0:T(8,128)(2,1)}), bf16[32,160,640]{2,1,0:T(8,128)(2,1)}, u32[]{:S(2)}, u32[]{:S(2)}) %all-to-all-start.15) | async-done | bytes 6553632 | tf_op jit(solution)/shard_map/all_to_all | solution.py:35
  3024.7 76.1 %all_to_all.398 = bf16[8,640,640]{2,0,1:T(8,128)(2,1)S(1)} all-to-all(bf16[8,640,640]{2,0,1:T(8,128)(2,1)S(1)} %copy.268), channel_id=1, replica_groups=mesh['data'=2,'dap2'=4,'dap'=4] {'dap'}, dimensions={1} | all-to-all | bytes 13107200 | tf_op jit(solution)/shard_map/all_to_all | solution.py:39
  3104.4 16.0 copy.271
  3141.1 213.0 %all-to-all-done.17 = bf16[32,160,640]{1,0,2:T(8,128)(2,1)} async-done(((bf16[32,160,640]{1,0,2:T(8,128)(2,1)}), bf16[32,160,640]{1,0,2:T(8,128)(2,1)}, u32[]{:S(2)}, u32[]{:S(2)}) %all-to-all-start.17) | async-done | bytes 6553632 | tf_op jit(solution)/shard_map/all_to_all | solution.py:40
  3354.1 15.4 copy.272
  3369.5 19.8 reshape.183
  3418.2 19.8 copy.326
  3438.1 18.6 convert_reduce_fusion
  3468.0 20.4 convolution_bitcast_fusion
  3488.4 22.9 fusion.29
  3511.3 15.1 copy.280
  3547.4 212.2 %all-to-all-done.18 = bf16[128,160,160]{2,1,0:T(8,128)(2,1)} async-done(((bf16[128,160,160]{2,1,0:T(8,128)(2,1)}), bf16[128,160,160]{2,1,0:T(8,128)(2,1)}, u32[]{:S(2)}, u32[]{:S(2)}) %all-to-all-start.18) | async-done | bytes 6553632 | tf_op jit(solution)/shard_map/all_to_all | solution.py:34
  3779.1 15.2 all_to_all.354
  3794.3 198.5 %all-to-all-done.20 = bf16[128,160,160]{2,1,0:T(8,128)(2,1)} async-done(((bf16[128,160,160]{2,1,0:T(8,128)(2,1)}), bf16[128,160,160]{2,1,0:T(8,128)(2,1)}, u32[]{:S(2)}, u32[]{:S(2)}) %all-to-all-start.20) | async-done | bytes 6553632 | tf_op jit(solution)/shard_map/all_to_all | solution.py:34
  4011.7 15.3 all_to_all.362
  4026.9 44.4 all-to-all-done.19
  4083.2 66.8 %all-to-all-done.21 = bf16[32,160,640]{2,1,0:T(8,128)(2,1)} async-done(((bf16[32,160,640]{2,1,0:T(8,128)(2,1)}), bf16[32,160,640]{2,1,0:T(8,128)(2,1)}, u32[]{:S(2)}, u32[]{:S(2)}) %all-to-all-start.21) | async-done | bytes 6553632 | tf_op jit(solution)/shard_map/all_to_all | solution.py:35
  4176.5 76.3 %all_to_all.399 = bf16[8,640,640]{2,0,1:T(8,128)(2,1)S(1)} all-to-all(bf16[8,640,640]{2,0,1:T(8,128)(2,1)S(1)} %copy.287), channel_id=1, replica_groups=mesh['data'=2,'dap2'=4,'dap'=4] {'dap'}, dimensions={1} | all-to-all | bytes 13107200 | tf_op jit(solution)/shard_map/all_to_all | solution.py:39
  4256.4 16.0 copy.290
  4292.9 213.1 %all-to-all-done.23 = bf16[32,160,640]{1,0,2:T(8,128)(2,1)} async-done(((bf16[32,160,640]{1,0,2:T(8,128)(2,1)}), bf16[32,160,640]{1,0,2:T(8,128)(2,1)}, u32[]{:S(2)}, u32[]{:S(2)}) %all-to-all-start.23) | async-done | bytes 6553632 | tf_op jit(solution)/shard_map/all_to_all | solution.py:40
  4506.1 15.4 copy.291
  4521.5 19.8 reshape.184
  4570.1 19.4 copy.327
  (182 shorter events, 647.8 us)
Async XLA Ops:
  0.0 20.1 slice-start
  0.0 19.3 copy-start.10
  0.0 19.4 copy-start.23
  0.0 19.4 copy-start.24
  2.1 18.0 slice-start.1
  19.4 18.3 copy-start.4
  75.8 235.3 %all-to-all-start = ((bf16[128,160,160]{2,1,0:T(8,128)(2,1)}), bf16[128,160,160]{2,1,0:T(8,128)(2,1)}, u32[]{:S(2)}, u32[]{:S(2)}) async-start(bf16[128,160,160]{2,1,0:T(8,128)(2,1)} %copy.224), calls=%async_computation | async-start | bytes 20971520 | tf_op jit(solution)/shard_map/all_to_all | solution.py:34
  311.1 233.3 %all-to-all-start.2 = ((bf16[128,160,160]{2,1,0:T(8,128)(2,1)}), bf16[128,160,160]{2,1,0:T(8,128)(2,1)}, u32[]{:S(2)}, u32[]{:S(2)}) async-start(bf16[128,160,160]{2,1,0:T(8,128)(2,1)} %copy.228), calls=%async_computation.2 | async-start | bytes 20971520 | tf_op jit(solution)/shard_map/all_to_all | solution.py:34
  544.4 78.5 %all-to-all-start.1 = ((bf16[32,160,640]{2,1,0:T(8,128)(2,1)}), bf16[32,160,640]{2,1,0:T(8,128)(2,1)}, u32[]{:S(2)}, u32[]{:S(2)}) async-start(bf16[32,160,640]{2,1,0:T(8,128)(2,1)} %all_to_all.291), calls=%async_computation.1 | async-start | bytes 13107200 | tf_op jit(solution)/shard_map/all_to_all | solution.py:35
  622.9 78.7 %all-to-all-start.3 = ((bf16[32,160,640]{2,1,0:T(8,128)(2,1)}), bf16[32,160,640]{2,1,0:T(8,128)(2,1)}, u32[]{:S(2)}, u32[]{:S(2)}) async-start(bf16[32,160,640]{2,1,0:T(8,128)(2,1)} %all_to_all.299), calls=%async_computation.3 | async-start | bytes 13107200 | tf_op jit(solution)/shard_map/all_to_all | solution.py:35
  634.9 70.4 %slice-start.2 = ((s8[6553600]{0:T(1024)(128)(4,1)}), s8[2359296]{0:T(1024)(128)(4,1)S(1)}, s32[]{:S(2)}) async-start(s8[6553600]{0:T(1024)(128)(4,1)} %bitcast.370), calls=%async_computation.26 | async-start | bytes 4718592
  701.6 4.1 slice-start.3
  816.1 6.3 copy-start.25
  816.1 6.3 copy-start.26
  816.1 233.6 %all-to-all-start.5 = ((bf16[32,160,640]{1,0,2:T(8,128)(2,1)}), bf16[32,160,640]{1,0,2:T(8,128)(2,1)}, u32[]{:S(2)}, u32[]{:S(2)}) async-start(bf16[32,160,640]{1,0,2:T(8,128)(2,1)} %copy.234), calls=%async_computation.5 | async-start | bytes 20971520 | tf_op jit(solution)/shard_map/all_to_all | solution.py:40
  1084.8 13.1 copy-start
  1142.0 30.0 copy-start.15
  1142.0 30.0 copy-start.16
  1172.0 20.4 copy-start.5
  1230.3 233.3 %all-to-all-start.6 = ((bf16[128,160,160]{2,1,0:T(8,128)(2,1)}), bf16[128,160,160]{2,1,0:T(8,128)(2,1)}, u32[]{:S(2)}, u32[]{:S(2)}) async-start(bf16[128,160,160]{2,1,0:T(8,128)(2,1)} %copy.243), calls=%async_computation.6 | async-start | bytes 20971520 | tf_op jit(solution)/shard_map/all_to_all | solution.py:34
  1463.6 233.2 %all-to-all-start.8 = ((bf16[128,160,160]{2,1,0:T(8,128)(2,1)}), bf16[128,160,160]{2,1,0:T(8,128)(2,1)}, u32[]{:S(2)}, u32[]{:S(2)}) async-start(bf16[128,160,160]{2,1,0:T(8,128)(2,1)} %copy.246), calls=%async_computation.8 | async-start | bytes 20971520 | tf_op jit(solution)/shard_map/all_to_all | solution.py:34
  1696.8 78.5 %all-to-all-start.7 = ((bf16[32,160,640]{2,1,0:T(8,128)(2,1)}), bf16[32,160,640]{2,1,0:T(8,128)(2,1)}, u32[]{:S(2)}, u32[]{:S(2)}) async-start(bf16[32,160,640]{2,1,0:T(8,128)(2,1)} %all_to_all.312), calls=%async_computation.7 | async-start | bytes 13107200 | tf_op jit(solution)/shard_map/all_to_all | solution.py:35
  1775.3 78.6 %all-to-all-start.9 = ((bf16[32,160,640]{2,1,0:T(8,128)(2,1)}), bf16[32,160,640]{2,1,0:T(8,128)(2,1)}, u32[]{:S(2)}, u32[]{:S(2)}) async-start(bf16[32,160,640]{2,1,0:T(8,128)(2,1)} %all_to_all.320), calls=%async_computation.9 | async-start | bytes 13107200 | tf_op jit(solution)/shard_map/all_to_all | solution.py:35
  1976.6 6.1 copy-start.9
  1976.6 6.3 copy-start.22
  1976.6 6.5 copy-start.21
  1976.6 233.6 %all-to-all-start.11 = ((bf16[32,160,640]{1,0,2:T(8,128)(2,1)}), bf16[32,160,640]{1,0,2:T(8,128)(2,1)}, u32[]{:S(2)}, u32[]{:S(2)}) async-start(bf16[32,160,640]{1,0,2:T(8,128)(2,1)} %copy.253), calls=%async_computation.11 | async-start | bytes 20971520 | tf_op jit(solution)/shard_map/all_to_all | solution.py:40
  2245.4 13.1 copy-start.1
  2293.9 29.9 copy-start.13
  2293.9 29.9 copy-start.14
  2323.8 20.4 copy-start.6
  2382.1 233.3 %all-to-all-start.12 = ((bf16[128,160,160]{2,1,0:T(8,128)(2,1)}), bf16[128,160,160]{2,1,0:T(8,128)(2,1)}, u32[]{:S(2)}, u32[]{:S(2)}) async-start(bf16[128,160,160]{2,1,0:T(8,128)(2,1)} %copy.262), calls=%async_computation.12 | async-start | bytes 20971520 | tf_op jit(solution)/shard_map/all_to_all | solution.py:34
  2615.4 233.6 %all-to-all-start.14 = ((bf16[128,160,160]{2,1,0:T(8,128)(2,1)}), bf16[128,160,160]{2,1,0:T(8,128)(2,1)}, u32[]{:S(2)}, u32[]{:S(2)}) async-start(bf16[128,160,160]{2,1,0:T(8,128)(2,1)} %copy.265), calls=%async_computation.14 | async-start | bytes 20971520 | tf_op jit(solution)/shard_map/all_to_all | solution.py:34
  2849.0 78.5 %all-to-all-start.13 = ((bf16[32,160,640]{2,1,0:T(8,128)(2,1)}), bf16[32,160,640]{2,1,0:T(8,128)(2,1)}, u32[]{:S(2)}, u32[]{:S(2)}) async-start(bf16[32,160,640]{2,1,0:T(8,128)(2,1)} %all_to_all.333), calls=%async_computation.13 | async-start | bytes 13107200 | tf_op jit(solution)/shard_map/all_to_all | solution.py:35
  2927.5 78.5 %all-to-all-start.15 = ((bf16[32,160,640]{2,1,0:T(8,128)(2,1)}), bf16[32,160,640]{2,1,0:T(8,128)(2,1)}, u32[]{:S(2)}, u32[]{:S(2)}) async-start(bf16[32,160,640]{2,1,0:T(8,128)(2,1)} %all_to_all.341), calls=%async_computation.15 | async-start | bytes 13107200 | tf_op jit(solution)/shard_map/all_to_all | solution.py:35
  2939.2 70.6 %slice-start.4 = ((s8[6553600]{0:T(1024)(128)(4,1)}), s8[2359296]{0:T(1024)(128)(4,1)S(1)}, s32[]{:S(2)}) async-start(s8[6553600]{0:T(1024)(128)(4,1)} %bitcast.374), calls=%async_computation.28 | async-start | bytes 4718592
  3006.0 4.1 slice-start.5
  3120.4 6.1 copy-start.20
  3120.4 6.3 copy-start.19
  3120.4 6.5 copy-start.8
  3120.4 233.6 %all-to-all-start.17 = ((bf16[32,160,640]{1,0,2:T(8,128)(2,1)}), bf16[32,160,640]{1,0,2:T(8,128)(2,1)}, u32[]{:S(2)}, u32[]{:S(2)}) async-start(bf16[32,160,640]{1,0,2:T(8,128)(2,1)} %copy.271), calls=%async_computation.17 | async-start | bytes 20971520 | tf_op jit(solution)/shard_map/all_to_all | solution.py:40
  3389.2 13.1 copy-start.2
  3438.1 29.9 copy-start.11
  3438.1 29.9 copy-start.12
  3468.0 20.4 copy-start.7
  3526.4 233.3 %all-to-all-start.18 = ((bf16[128,160,160]{2,1,0:T(8,128)(2,1)}), bf16[128,160,160]{2,1,0:T(8,128)(2,1)}, u32[]{:S(2)}, u32[]{:S(2)}) async-start(bf16[128,160,160]{2,1,0:T(8,128)(2,1)} %copy.280), calls=%async_computation.18 | async-start | bytes 20971520 | tf_op jit(solution)/shard_map/all_to_all | solution.py:34
  3759.6 233.2 %all-to-all-start.20 = ((bf16[128,160,160]{2,1,0:T(8,128)(2,1)}), bf16[128,160,160]{2,1,0:T(8,128)(2,1)}, u32[]{:S(2)}, u32[]{:S(2)}) async-start(bf16[128,160,160]{2,1,0:T(8,128)(2,1)} %copy.283), calls=%async_computation.20 | async-start | bytes 20971520 | tf_op jit(solution)/shard_map/all_to_all | solution.py:34
  3992.9 78.5 %all-to-all-start.19 = ((bf16[32,160,640]{2,1,0:T(8,128)(2,1)}), bf16[32,160,640]{2,1,0:T(8,128)(2,1)}, u32[]{:S(2)}, u32[]{:S(2)}) async-start(bf16[32,160,640]{2,1,0:T(8,128)(2,1)} %all_to_all.354), calls=%async_computation.19 | async-start | bytes 13107200 | tf_op jit(solution)/shard_map/all_to_all | solution.py:35
  4071.4 78.6 %all-to-all-start.21 = ((bf16[32,160,640]{2,1,0:T(8,128)(2,1)}), bf16[32,160,640]{2,1,0:T(8,128)(2,1)}, u32[]{:S(2)}, u32[]{:S(2)}) async-start(bf16[32,160,640]{2,1,0:T(8,128)(2,1)} %all_to_all.362), calls=%async_computation.21 | async-start | bytes 13107200 | tf_op jit(solution)/shard_map/all_to_all | solution.py:35
  4272.4 6.1 copy-start.18
  4272.4 6.3 copy-start.17
  4272.4 233.6 %all-to-all-start.23 = ((bf16[32,160,640]{1,0,2:T(8,128)(2,1)}), bf16[32,160,640]{1,0,2:T(8,128)(2,1)}, u32[]{:S(2)}, u32[]{:S(2)}) async-start(bf16[32,160,640]{1,0,2:T(8,128)(2,1)} %copy.290), calls=%async_computation.23 | async-start | bytes 20971520 | tf_op jit(solution)/shard_map/all_to_all | solution.py:40
  4541.2 13.1 copy-start.3
where the time goes:
time: 4630 us; the launch traced here: 4600 us
  waiting for transfers between devices  2940 us (63%)
  local copies, waits for them, and re-layouts  745 us (16%)
  blocking collectives  305 us (7%)
  other arithmetic  248 us (5%)
  matrix products  248 us (5%)
  starting transfers between devices  116 us (3%)
    all_to_all x8, waiting for transfers between devices, to_channels(): col_full = lax.all_to_all(block, 'dap2', 0, 2, tiled=True)  1640 us
    all_to_all x4, waiting for transfers between devices, from_channels(): return lax.all_to_all(row_part, 'dap2', 2, 0, tiled=True)  852 us
    all_to_all x8, waiting for transfers between devices, to_channels(): return lax.all_to_all(col_full, 'dap', 0, 1, tiled=True)  445 us
    all_to_all x4, blocking collectives, from_channels(): row_part = lax.all_to_all(block, 'dap', 1, 0, tiled=True)  305 us
    all_to_all x16, local copies, waits for them, and re-layouts, to_channels(): col_full = lax.all_to_all(block, 'dap2', 0, 2, tiled=True)  230 us
  transfers between devices with their start and end apart: 20, of which 20 were waited for; matrix products, arithmetic and copies ran while one was open for 5% of the time, Pallas kernels for 0%

commit v1 on v0

v1 whole, which is shorter than its diff:
```python
import functools

import jax
import jax.numpy as jnp
from jax import lax
from jax.experimental import pallas as pl
from jax.experimental.pallas import tpu as pltpu
from jax.sharding import PartitionSpec as P

NORM_EPS = 1e-5
F32 = jnp.float32
BF16 = jnp.bfloat16
MESH = pl.DeviceIdType.MESH
ND = 16
CPD = 8
B = 160
GR = 4
RR = 40
SL = 8
STEPS = RR // SL
SWAP = 136


def to_tiles(block):
    rest = block.shape[2:]
    grouped = block.reshape((GR, RR, B) + rest)
    main = grouped[:, :, :128]
    rem = jnp.swapaxes(grouped[:, :, 128:], 0, 1).reshape((1, RR, 128) + rest)
    return jnp.concatenate([main, jnp.swapaxes(rem, 0, 0)], axis=0)


def from_tiles(tiles):
    rest = tiles.shape[3:]
    main = tiles[:GR]
    rem = jnp.swapaxes(tiles[GR].reshape((RR, GR, 32) + rest), 0, 1)
    return jnp.concatenate([main, rem], axis=2).reshape((B, B) + rest)


def sigmoid(v):
    return 0.5 * jnp.tanh(0.5 * v) + 0.5


def norm_lanes(values, gamma, beta):
    centered = values - jnp.mean(values, axis=-1, keepdims=True)
    variance = jnp.mean(centered * centered, axis=-1, keepdims=True)
    return centered * lax.rsqrt(variance + NORM_EPS) * gamma + beta


def my_place():
    row, col = lax.axis_index('dap'), lax.axis_index('dap2')
    return row, col, row * 4 + col


def partner(me, n):
    other = lax.rem(me + n, ND)
    return other, {'dap': other // 4, 'dap2': lax.rem(other, 4)}


def greet(me):
    barrier = pltpu.get_barrier_semaphore()

    def signal(n, carry):
        _, device = partner(me, n)
        pl.semaphore_signal(barrier, inc=1, device_id=device, device_id_type=MESH)
        return carry

    lax.fori_loop(1, ND, signal, 0)
    return barrier


def position_kernel(finish, project, *refs):
    refs = list(refs)
    take = lambda: refs.pop(0)
    z_ref = take()
    if finish:
        t_ref, gin_ref, bin_ref, wg_ref, gout_ref, bout_ref, wo_ref = [take() for _ in range(7)]
    if project:
        mask_ref, gnext_ref, bnext_ref, wp_ref = [take() for _ in range(4)]
    if finish:
        zo_ref = take()
    if project:
        a_in, b_in = take(), take()
    if finish:
        y_buf = take()
    if project:
        sa, sb, out_a, out_b, send_sem, recv_sem = [take() for _ in range(6)]
    s = pl.program_id(0)
    if project:
        row, col, me = my_place()
        barrier = pltpu.get_barrier_semaphore()

        @pl.when(s == 0)
        def _():
            greet(me)

    def group(grp, carry):
        if finish:
            total = jnp.zeros((SL, 128), F32)
            for cb in range(8):
                total += jnp.sum(t_ref[cb * 16:(cb + 1) * 16, grp].astype(F32), axis=0)
            mean = (total * (1.0 / 128))[None]
            total = jnp.zeros((SL, 128), F32)
            for cb in range(8):
                centered = t_ref[cb * 16:(cb + 1) * 16, grp].astype(F32) - mean
                total += jnp.sum(centered * centered, axis=0)
            scale = lax.rsqrt(total * (1.0 / 128) + NORM_EPS)[None]
            for cb in range(8):
                sl = slice(cb * 16, (cb + 1) * 16)
                y = (t_ref[sl, grp].astype(F32) - mean) * scale * gout_ref[sl] + bout_ref[sl]
                y_buf[cb * 128:(cb + 1) * 128, :] = y.reshape(128, 128)

        def tile(r, inner):
            zf = z_ref[grp, r].astype(F32)
            if finish:
                x = norm_lanes(zf, gin_ref[...], bin_ref[...]).astype(BF16)
                gate = sigmoid(jnp.dot(x, wg_ref[...], preferred_element_type=F32))
                y = y_buf[pl.ds(r, 128, stride=SL), :].astype(BF16)
                update = lax.dot_general(y, wo_ref[...], (((0,), (0,)), ((), ())), preferred_element_type=F32)
                znew = (zf + gate * update).astype(BF16)
                zo_ref[grp, r] = znew
                zf = znew.astype(F32)
            if project:
                x = norm_lanes(zf, gnext_ref[...], bnext_ref[...]).astype(BF16)
                q = lax.dot_general(wp_ref[...], x, (((1,), (1,)), ((), ())), preferred_element_type=F32)
                m = mask_ref[grp, pl.ds(r, 1), :]
                base = pl.multiple_of(r * SWAP, 8)
                sa[pl.ds(base, 128), :] = m * sigmoid(q[128:256]) * q[:128]
                sb[pl.ds(base, 128), :] = m * sigmoid(q[384:]) * q[256:384]
            return inner

        lax.fori_loop(0, SL, tile, 0, unroll=2)

        if project:
            def swap(cb, inner):
                for u in range(8):
                    c = cb * 8 + u
                    out_a[s, c, grp] = sa[pl.ds(c, SL, stride=SWAP), :].astype(BF16)
                    out_b[s, c, grp] = sb[pl.ds(c, SL, stride=SWAP), :].astype(BF16)
                return inner

            lax.fori_loop(0, 16, swap, 0)
        return carry

    lax.fori_loop(0, 5, group, 0)

    if project:
        @pl.when(s == 0)
        def _():
            pl.semaphore_wait(barrier, ND - 1)

        rows = pl.ds(pl.multiple_of(s * SL, SL), SL)
        lanes = pl.ds(pl.multiple_of(col * 128, 128), 128)

        def send(n, carry):
            other, device = partner(me, n)
            chans = pl.ds(other * CPD, CPD)
            for k, (src, dst) in enumerate(((out_a, a_in), (out_b, b_in))):
                pltpu.make_async_remote_copy(
                    src_ref=src.at[s, chans], dst_ref=dst.at[:, row, :, rows, lanes],
                    send_sem=send_sem.at[k], recv_sem=recv_sem.at[k],
                    device_id=device, device_id_type=MESH).start()
            return carry

        lax.fori_loop(1, ND, send, 0)
        for k, (src, dst) in enumerate(((out_a, a_in), (out_b, b_in))):
            pltpu.make_async_copy(src.at[s, pl.ds(me * CPD, CPD)], dst.at[:, row, :, rows, lanes], recv_sem.at[k]).start()

        @pl.when(s == STEPS - 1)
        def _():
            for k, (src, dst) in enumerate(((out_a, a_in), (out_b, b_in))):
                pltpu.make_async_copy(dst, dst, recv_sem.at[k]).wait()
                sent = src.at[:, pl.ds(0, 128 - CPD)]
                pltpu.make_async_copy(sent, sent, send_sem.at[k]).wait()


def position_call(z_tiles, finish_args, project_args, collective_id):
    finish, project = finish_args is not None, project_args is not None
    full = lambda arr: pl.BlockSpec(arr.shape, lambda s: (0,) * arr.ndim)
    z_spec = pl.BlockSpec((5, SL, 128, 128), lambda s: (0, s, 0, 0))
    args, specs = [z_tiles], [z_spec]
    outs, out_specs, scratch = [], [], []
    if finish:
        args += list(finish_args)
        specs += [pl.BlockSpec((128, 5, SL, 128), lambda s: (0, 0, s, 0))] + [full(v) for v in finish_args[1:]]
        outs.append(jax.ShapeDtypeStruct(z_tiles.shape, BF16))
        out_specs.append(z_spec)
        scratch.append(pltpu.VMEM((128 * SL, 128), F32))
    if project:
        args += list(project_args)
        specs += [pl.BlockSpec((5, SL, 128), lambda s: (0, s, 0))] + [full(v) for v in project_args[1:]]
        outs += [jax.ShapeDtypeStruct((CPD, 4, 5, RR, 512), BF16)] * 2
        out_specs += [pl.BlockSpec(memory_space=pl.ANY)] * 2
        scratch += [pltpu.VMEM((SWAP * SL, 128), F32)] * 2
        scratch += [pltpu.VMEM((STEPS, 128, 5, SL, 128), BF16)] * 2
        scratch += [pltpu.SemaphoreType.DMA((2,)), pltpu.SemaphoreType.DMA((2,))]
    params = dict(dimension_semantics=('arbitrary',), vmem_limit_bytes=60 * 2 ** 20)
    if project:
        params.update(collective_id=collective_id, has_side_effects=True)
    name = 'position' + ('_finish' if finish else '') + ('_project' if project else '')
    return pl.pallas_call(
        functools.partial(position_kernel, finish, project), name=name, grid=(STEPS,),
        in_specs=specs, out_specs=out_specs, out_shape=outs, scratch_shapes=scratch,
        compiler_params=pltpu.CompilerParams(**params))(*args)


def channel_kernel(incoming, a_ref, b_ref, perm_ref, t_in, amat, bmat, tmat, t_out, send_sem, recv_sem):
    c = pl.program_id(0)
    row, col, me = my_place()
    barrier = pltpu.get_barrier_semaphore()

    @pl.when(c == 0)
    def _():
        greet(me)

    def rem_columns(ref):
        packed = ref[0, :, B:, :].astype(F32).reshape(4 * RR, 512).astype(BF16)
        return jnp.dot(packed, perm_ref[...], preferred_element_type=F32)

    def natural(wide, blk):
        return jnp.concatenate([wide[blk * RR:(blk + 1) * RR, g * 128:(g + 1) * 128] for g in range(GR)], axis=0)

    wide = rem_columns(a_ref)
    for blk in range(4):
        amat[blk * B:(blk + 1) * B, :512] = a_ref[0, blk, :B, :]
        amat[blk * B:(blk + 1) * B, 512:] = natural(wide, blk).astype(BF16)
    wide = rem_columns(b_ref)
    for blk in range(4):
        if incoming:
            bmat[blk * B:(blk + 1) * B, :512] = b_ref[0, blk, :B, :]
            bmat[blk * B:(blk + 1) * B, 512:] = natural(wide, blk).astype(BF16)
        else:
            last = natural(wide, blk).astype(BF16)
            bmat[blk * 128:(blk + 1) * 128, :512] = b_ref[0, blk, :128, :]
            bmat[512 + blk * 32:512 + (blk + 1) * 32, :512] = b_ref[0, blk, 128:B, :]
            bmat[blk * 128:(blk + 1) * 128, 512:] = last[:128]
            bmat[512 + blk * 32:512 + (blk + 1) * 32, 512:] = last[128:]
    contract = 0 if incoming else 1
    tmat[...] = lax.dot_general(amat[...], bmat[...], (((contract,), (contract,)), ((), ())), preferred_element_type=F32)

    def rows_of(blk, lanes):
        if incoming:
            return jnp.concatenate([tmat[blk * 128:(blk + 1) * 128, lanes], tmat[512 + blk * 32:512 + (blk + 1) * 32, lanes]], axis=0)
        return tmat[blk * B:(blk + 1) * B, lanes]

    packed = []
    for blk in range(4):
        for j in range(4):
            t_out[c, blk * 4 + j, :B, :] = rows_of(blk, slice(j * 128, (j + 1) * 128)).astype(BF16)
        rem = rows_of(blk, slice(512, 640))
        packed.append(jnp.concatenate([rem[g * RR:(g + 1) * RR] for g in range(GR)], axis=1))
    wide = jnp.dot(jnp.concatenate(packed, axis=0).astype(BF16), perm_ref[...], preferred_element_type=F32)
    for blk in range(4):
        for j in range(4):
            t_out[c, blk * 4 + j, B:, :] = wide[blk * RR:(blk + 1) * RR, j * 128:(j + 1) * 128].astype(BF16)

    @pl.when(c == 0)
    def _():
        pl.semaphore_wait(barrier, ND - 1)

    def send(n, carry):
        other, device = partner(me, n)
        pltpu.make_async_remote_copy(
            src_ref=t_out.at[c, other], dst_ref=t_in.at[me * CPD + c],
            send_sem=send_sem, recv_sem=recv_sem, device_id=device, device_id_type=MESH).start()
        return carry

    lax.fori_loop(1, ND, send, 0)
    pltpu.make_async_copy(t_out.at[c, me], t_in.at[me * CPD + c], recv_sem).start()

    @pl.when(c == CPD - 1)
    def _():
        pltpu.make_async_copy(t_in, t_in, recv_sem).wait()
        sent = t_out.at[:, pl.ds(0, ND - 1)]
        pltpu.make_async_copy(sent, sent, send_sem).wait()


def channel_call(a_in, b_in, perm, incoming):
    spec = pl.BlockSpec((1, 4, 200, 512), lambda c: (c, 0, 0, 0))
    return pl.pallas_call(
        functools.partial(channel_kernel, incoming), name='channel_in' if incoming else 'channel_out', grid=(CPD,),
        in_specs=[spec, spec, pl.BlockSpec((512, 512), lambda c: (0, 0))],
        out_specs=pl.BlockSpec(memory_space=pl.ANY),
        out_shape=jax.ShapeDtypeStruct((128, 200, 128), BF16),
        scratch_shapes=[
            pltpu.VMEM((640, 640), BF16), pltpu.VMEM((640, 640), BF16), pltpu.VMEM((640, 640), F32),
            pltpu.VMEM((CPD, ND, 200, 128), BF16),
            pltpu.SemaphoreType.DMA, pltpu.SemaphoreType.DMA],
        compiler_params=pltpu.CompilerParams(
            dimension_semantics=('arbitrary',), vmem_limit_bytes=60 * 2 ** 20,
            collective_id=4 if incoming else 3, has_side_effects=True),
    )(a_in.reshape(CPD, 4, 200, 512), b_in.reshape(CPD, 4, 200, 512), perm)


def solution(mesh):
    pair_spec = P(('data', 'dap'), 'dap2', None)
    mask_spec = P(('data', 'dap'), 'dap2')

    def local_fn(pair_act, pair_mask, in_gamma, in_beta, w_proj, w_gate, out_gamma, out_beta, w_out):
        mask = to_tiles(pair_mask.astype(F32))
        z = to_tiles(pair_act)
        src = jnp.arange(512)
        perm = (((src % 128) // 32 * 128 + src // 128 * 32 + src % 32)[:, None] == jnp.arange(512)[None, :]).astype(BF16)
        updates = [(layer, u) for layer in range(in_gamma.shape[0]) for u in range(2)]

        def project_args(at):
            return (mask, in_gamma[at][None], in_beta[at][None], w_proj[at].T)

        def finish_args(at, t):
            wide = lambda v: jnp.broadcast_to(v[at][:, None, None], (128, 1, 128))
            return (t.reshape(128, 5, RR, 128), in_gamma[at][None], in_beta[at][None], w_gate[at], wide(out_gamma), wide(out_beta), w_out[at])

        a_in, b_in = position_call(z, None, project_args(updates[0]), 1)
        for n, at in enumerate(updates):
            t = channel_call(a_in, b_in, perm, at[1] == 1)
            if n + 1 < len(updates):
                z, a_in, b_in = position_call(z, finish_args(at, t), project_args(updates[n + 1]), 2)
            else:
                z, = position_call(z, finish_args(at, t), None, None)
        return from_tiles(z)

    return jax.shard_map(local_fn, mesh=mesh, in_specs=(pair_spec, mask_spec) + (P(),) * 7, out_specs=pair_spec, check_vma=False)
```

time: 4630 us -> 1880 us (0.41)
  waiting for transfers between devices: 2940 us -> 0 us
  Pallas kernels: 0 us -> 1840 us
  local copies, waits for them, and re-layouts: 745 us -> 20.8 us
  blocking collectives: 305 us -> 0 us
  matrix products: 248 us -> 0 us
  other arithmetic: 248 us -> 11.6 us
  starting transfers between devices: 116 us -> 0 us
    all_to_all x20 -> x0, waiting for transfers between devices: 2940 us -> none  [the longest x8 1640 us: to_channels(): col_full = lax.all_to_all(block, 'dap2', 0, 2, tiled=True)]
    pallas_call x0 -> x9, Pallas kernels: none -> 1840 us  [the longest x5 1240 us: position_call(): pl.pallas_call(functools.partial(position_kernel, finish, project), name=...]
    all_to_all x36 -> x0, local copies, waits for them, and re-layouts: 416 us -> none  [the longest x16 230 us: to_channels(): col_full = lax.all_to_all(block, 'dap2', 0, 2, tiled=True)]
    all_to_all x4 -> x0, blocking collectives: 305 us -> none  [from_channels(): row_part = lax.all_to_all(block, 'dap', 1, 0, tiled=True)]
    convert_element_type x20 -> x0, local copies, waits for them, and re-layouts: 305 us -> none  [the longest x4 79.1 us: finish_local(): tri_blk.astype(jnp.float32)]
    dot_general x16 -> x0, matrix products: 248 us -> none  [the longest x4 78.9 us: project_local(): jnp.einsum('ijd,dgc->gcij', normed, w_proj.reshape(w_proj.shape[0], 4, tr...]
    convert_element_type x9 -> x2, other arithmetic: 137 us -> 1.88 us  [the longest x1 0.95 us: local_fn(): ((src % 128 // 32 * 128 + src // 128 * 32 + src % 32)[:, None] == jnp.ara...]
    all_to_all x20 -> x0, starting transfers between devices: 116 us -> none  [the longest x8 48.7 us: to_channels(): col_full = lax.all_to_all(block, 'dap2', 0, 2, tiled=True)]
  transfers between devices with their start and end apart: 20 -> 0, of which waited for: 20 -> 0; matrix products, arithmetic and copies ran while one was open for 5% -> 0% of each run, Pallas kernels for 0% -> 0%
where the time goes in v1:
time: 1880 us
  Pallas kernels  1840 us (98%)
  local copies, waits for them, and re-layouts  20.8 us (1%)
    pallas_call x5, Pallas kernels, position_call(): pl.pallas_call(functools.partial(position_kernel, finish, project), name=...  1240 us
    pallas_call x4, Pallas kernels, channel_call(): pl.pallas_call(functools.partial(channel_kernel, incoming), name='channel...  608 us

profile of v1, /device:TPU:0, one launch (start us, length us, event | category | flops | bytes accessed | tf_op | source)
XLA Modules:
  0.0 1877.2 jit_solution(1613957511763641950)
XLA Ops:
  0.0 1.4 slice_bitcast_fusion.12
  1.4 0.9 convert_element_type.12
  2.4 0.1 reshape.124
  2.5 0.6 pad_maximum_fusion.2.refs_1_.refs_8_
  3.2 3.6 slice.144
  6.8 1.6 slice_bitcast_fusion
  8.3 0.4 copy.17
  8.7 0.0 copy-start
  8.8 3.4 pad_maximum_fusion.refs_0_
  12.1 0.0 copy-done
  12.1 0.8 copy.24
  12.9 293.6 %position_project.1 = (bf16[8,4,5,40,512]{4,3,2,1,0:T(8,128)(2,1)}, bf16[8,4,5,40,512]{4,3,2,1,0:T(8,128)(2,1)}) custom-call(bf16[5,40,128,128]{3,2,1,0:T(8,128)(2,1)} %pad_maximum_fusion.refs_0_, f32[5,40,128]{2,1,0:T(8,128)} %pad_maximum_fusion.2.refs_1_.refs_8_, f32[1,128]{1,0:T(1,128)} %get-tuple-element.56.refs_2_, f32[1,128]{1,0:T(1,128)} %get-tuple-element.49.refs_3_, ...), custom_call_target="tpu_custom_call" | custom-call | tf_op jit(solution)/shard_map/position_project/pallas_call | solution.py:200
  306.6 1.0 fusion.perm_ref
  307.5 0.0 copy-start.1
  307.5 0.0 copy-start.2
  307.5 0.0 copy-start.3
  307.5 0.0 copy-start.4
  307.5 150.9 %channel_out.2 = bf16[128,200,128]{2,1,0:T(8,128)(2,1)} custom-call(bf16[8,4,200,512]{3,2,1,0:T(8,128)(2,1)} %bitcast.97, bf16[8,4,200,512]{3,2,1,0:T(8,128)(2,1)} %bitcast.98, bf16[512,512]{1,0:T(8,128)(2,1)} %fusion.perm_ref), custom_call_target="tpu_custom_call" | custom-call | tf_op jit(solution)/shard_map/channel_out/pallas_call | solution.py:279
  458.5 0.0 copy-done.1
  458.5 0.0 copy-done.2
  458.5 0.7 slice_bitcast_fusion.2
  459.2 0.8 copy.25
  460.0 0.0 copy-done.3
  460.0 0.8 broadcast_in_dim.59.refs_5_
  460.8 0.0 copy-done.4
  460.8 0.8 broadcast_in_dim.61.refs_6_
  461.6 299.6 %position_finish_project.3 = (bf16[5,40,128,128]{3,2,1,0:T(8,128)(2,1)}, bf16[8,4,5,40,512]{4,3,2,1,0:T(8,128)(2,1)}, bf16[8,4,5,40,512]{4,3,2,1,0:T(8,128)(2,1)}) custom-call(bf16[5,40,128,128]{3,2,1,0:T(8,128)(2,1)} %pad_maximum_fusion.refs_0_, bf16[128,5,40,128]{3,2,1,0:T(8,128)(2,1)} %bitcast.84, f32[1,128]{1,0:T(1,128)} %get-tuple-element.56.refs_2_, ...), custom_call_target="tpu_custom_call" | custom-call | tf_op jit(solution)/shard_map/position_finish_project/pallas_call | solution.py:200
  761.2 153.3 %channel_in.2 = bf16[128,200,128]{2,1,0:T(8,128)(2,1)} custom-call(bf16[8,4,200,512]{3,2,1,0:T(8,128)(2,1)} %bitcast.93, bf16[8,4,200,512]{3,2,1,0:T(8,128)(2,1)} %bitcast.94, bf16[512,512]{1,0:T(8,128)(2,1)} %fusion.perm_ref), custom_call_target="tpu_custom_call" | custom-call | tf_op jit(solution)/shard_map/channel_in/pallas_call | solution.py:279
  914.5 0.8 copy.26
  915.3 0.8 broadcast_in_dim.63.refs_5_
  916.1 0.8 broadcast_in_dim.65.refs_6_
  916.9 300.6 %position_finish_project.4 = (bf16[5,40,128,128]{3,2,1,0:T(8,128)(2,1)}, bf16[8,4,5,40,512]{4,3,2,1,0:T(8,128)(2,1)}, bf16[8,4,5,40,512]{4,3,2,1,0:T(8,128)(2,1)}) custom-call(bf16[5,40,128,128]{3,2,1,0:T(8,128)(2,1)} %get-tuple-element.18.refs_0_, bf16[128,5,40,128]{3,2,1,0:T(8,128)(2,1)} %bitcast.86, f32[1,128]{1,0:T(1,128)} %get-tuple-element.57.refs_9_.refs_2_, ...), custom_call_target="tpu_custom_call" | custom-call | tf_op jit(solution)/shard_map/position_finish_project/pallas_call | solution.py:200
  1217.5 151.2 %channel_out.3 = bf16[128,200,128]{2,1,0:T(8,128)(2,1)} custom-call(bf16[8,4,200,512]{3,2,1,0:T(8,128)(2,1)} %bitcast.95, bf16[8,4,200,512]{3,2,1,0:T(8,128)(2,1)} %bitcast.96, bf16[512,512]{1,0:T(8,128)(2,1)} %fusion.perm_ref), custom_call_target="tpu_custom_call" | custom-call | tf_op jit(solution)/shard_map/channel_out/pallas_call | solution.py:279
  1368.7 0.8 copy.27
  1369.5 0.8 broadcast_in_dim.67.refs_5_
  1370.3 0.8 broadcast_in_dim.69.refs_6_
  1371.1 299.8 %position_finish_project.5 = (bf16[5,40,128,128]{3,2,1,0:T(8,128)(2,1)}, bf16[8,4,5,40,512]{4,3,2,1,0:T(8,128)(2,1)}, bf16[8,4,5,40,512]{4,3,2,1,0:T(8,128)(2,1)}) custom-call(bf16[5,40,128,128]{3,2,1,0:T(8,128)(2,1)} %get-tuple-element.21.refs_0_, bf16[128,5,40,128]{3,2,1,0:T(8,128)(2,1)} %bitcast.85, f32[1,128]{1,0:T(1,128)} %get-tuple-element.55.refs_9_.refs_2_, ...), custom_call_target="tpu_custom_call" | custom-call | tf_op jit(solution)/shard_map/position_finish_project/pallas_call | solution.py:200
  1670.9 152.2 %channel_in.3 = bf16[128,200,128]{2,1,0:T(8,128)(2,1)} custom-call(bf16[8,4,200,512]{3,2,1,0:T(8,128)(2,1)} %bitcast.91, bf16[8,4,200,512]{3,2,1,0:T(8,128)(2,1)} %bitcast.92, bf16[512,512]{1,0:T(8,128)(2,1)} %fusion.perm_ref), custom_call_target="tpu_custom_call" | custom-call | tf_op jit(solution)/shard_map/channel_in/pallas_call | solution.py:279
  1823.1 0.8 broadcast_in_dim.71.refs_5_
  1823.9 0.8 broadcast_in_dim.73.refs_6_
  1824.7 43.4 %position_finish.1 = bf16[5,40,128,128]{3,2,1,0:T(8,128)(2,1)} custom-call(bf16[5,40,128,128]{3,2,1,0:T(8,128)(2,1)} %get-tuple-element.24.refs_0_, bf16[128,5,40,128]{3,2,1,0:T(8,128)(2,1)} %bitcast.87, f32[1,128]{1,0:T(1,128)} %get-tuple-element.58.refs_9_.refs_2_, f32[1,128]{1,0:T(1,128)} %get-tuple-element.47.refs_10_.refs_3_, ...), custom_call_target="tpu_custom_call" | custom-call | tf_op jit(solution)/shard_map/position_finish/pallas_call | solution.py:200
  1868.1 0.0 slice-start.1
  1868.1 0.0 slice-start
  1868.1 1.3 slice-done.1
  1869.5 1.3 copy.29
  1870.8 0.7 slice-done
  1871.5 5.7 pad_maximum_fusion.1
  (7 shorter events, 0.1 us)
Async XLA Ops:
  8.7 3.4 copy-start
  307.5 151.0 %copy-start.1 = (bf16[2,2,128,128]{3,2,1,0:T(8,128)(2,1)S(1)}, bf16[2,2,128,128]{3,2,1,0:T(8,128)(2,1)}, u32[]{:S(2)}) copy-start(bf16[2,2,128,128]{3,2,1,0:T(8,128)(2,1)} %param.17) | copy-start | bytes 393220
  307.5 151.0 %copy-start.2 = (bf16[2,2,128,128]{3,2,1,0:T(8,128)(2,1)S(1)}, bf16[2,2,128,128]{3,2,1,0:T(8,128)(2,1)}, u32[]{:S(2)}) copy-start(bf16[2,2,128,128]{3,2,1,0:T(8,128)(2,1)} %param.14) | copy-start | bytes 393220
  307.5 152.5 %copy-start.3 = (f32[2,2,128]{2,1,0:T(2,128)S(1)}, f32[2,2,128]{2,1,0:T(2,128)}, u32[]{:S(2)}) copy-start(f32[2,2,128]{2,1,0:T(2,128)} %param.15) | copy-start | bytes 6148
  307.5 153.3 %copy-start.4 = (f32[2,2,128]{2,1,0:T(2,128)S(1)}, f32[2,2,128]{2,1,0:T(2,128)}, u32[]{:S(2)}) copy-start(f32[2,2,128]{2,1,0:T(2,128)} %param.16) | copy-start | bytes 6148
  1868.1 1.3 slice-start.1
  1868.1 3.4 slice-start

commit v2 on v1

v2 whole, which is shorter than its diff:
```python
import functools

import jax
import jax.numpy as jnp
from jax import lax
from jax.experimental import pallas as pl
from jax.experimental.pallas import tpu as pltpu
from jax.sharding import PartitionSpec as P

NORM_EPS = 1e-5
F32 = jnp.float32
BF16 = jnp.bfloat16
MESH = pl.DeviceIdType.MESH
ND = 16
B = 160
GR = 4
RR = 40
SL = 8
STEPS = RR // SL
UNROLL = 4
SWAP = 136


def to_tiles(block):
    rest = block.shape[2:]
    grouped = block.reshape((GR, RR, B) + rest)
    main = grouped[:, :, :128]
    rem = jnp.swapaxes(grouped[:, :, 128:], 0, 1).reshape((1, RR, 128) + rest)
    return jnp.concatenate([main, rem], axis=0)


def sigmoid(v):
    return 0.5 * jnp.tanh(0.5 * v) + 0.5


def norm_lanes(values, gamma, beta):
    centered = values - jnp.mean(values, axis=-1, keepdims=True)
    variance = jnp.mean(centered * centered, axis=-1, keepdims=True)
    return centered * lax.rsqrt(variance + NORM_EPS) * gamma + beta


def place(team):
    row, col = lax.axis_index('dap'), lax.axis_index('dap2')
    return row * 4 + col if team == ND else row * 2 + lax.rem(col, 2)


def partner(team, n):
    other = lax.rem(place(team) + n, team)
    if team == ND:
        return other, {'dap': other // 4, 'dap2': lax.rem(other, 4)}
    half = lax.axis_index('dap2') // 2
    return other, {'dap': other // 2, 'dap2': half * 2 + lax.rem(other, 2)}


def greet(team):
    barrier = pltpu.get_barrier_semaphore()

    def signal(n, carry):
        _, device = partner(team, n)
        pl.semaphore_signal(barrier, inc=1, device_id=device, device_id_type=MESH)
        return carry

    lax.fori_loop(1, team, signal, 0)


def position_kernel(finish, project, natural_in, *refs):
    refs = list(refs)
    take = lambda: refs.pop(0)
    z_in = take()
    if finish:
        t_ref, gin_ref, bin_ref, wg_ref, gout_ref, bout_ref, wo_ref = [take() for _ in range(7)]
    if project:
        mask_ref, gnext_ref, bnext_ref, wp_ref = [take() for _ in range(4)]
    if finish:
        z_out = take()
    if project:
        a_in, b_in = take(), take()
    natural_out = not project
    z_ref = take() if natural_in else z_in
    if finish:
        y_buf = take()
        zo_ref = take() if natural_out else z_out
    if project:
        sa, sb, out_a, out_b, send_sem, recv_sem = [take() for _ in range(6)]
    s = pl.program_id(0)
    if project:
        @pl.when(s == 0)
        def _():
            greet(ND)

        row, col = lax.axis_index('dap'), lax.axis_index('dap2')
        rows = pl.ds(pl.multiple_of(s * SL, SL), SL)

        def push(grp):
            for k, (src, dst) in enumerate(((out_a, a_in), (out_b, b_in))):
                team = 8 if project == 'in' and k == 1 else ND
                split = 8 if project == 'in' else ND
                each = 128 // split
                lane = col if team == ND else lax.rem(col, 2)
                lanes = pl.ds(pl.multiple_of(lane * 128, 128), 128)
                there = dst.at[:, row, grp, rows, lanes]

                def part(index):
                    return src.at[s, pl.ds(index * each, each), grp]

                def send(n, carry):
                    other, device = partner(team, n)
                    if team != split:
                        other = device['dap'] * 2 + lax.rem(device['dap2'], 2)
                    pltpu.make_async_remote_copy(
                        src_ref=part(other), dst_ref=there, send_sem=send_sem.at[k], recv_sem=recv_sem.at[k],
                        device_id=device, device_id_type=MESH).start()
                    return carry

                lax.fori_loop(1, team, send, 0)
                pltpu.make_async_copy(part(place(split)), there, recv_sem.at[k]).start()

    if natural_in:
        def load(r, carry):
            for g in range(GR):
                z_ref[g, r] = z_in[g, r, :128]
                z_ref[GR, r, g * 32:(g + 1) * 32] = z_in[g, r, 128:]
            return carry

        lax.fori_loop(0, SL, load, 0)

    def group(grp, carry):
        if finish:
            total = jnp.zeros((SL, 128), F32)
            for cb in range(8):
                total += jnp.sum(t_ref[cb * 16:(cb + 1) * 16, grp].astype(F32), axis=0)
            mean = (total * (1.0 / 128))[None]
            total = jnp.zeros((SL, 128), F32)
            for cb in range(8):
                centered = t_ref[cb * 16:(cb + 1) * 16, grp].astype(F32) - mean
                total += jnp.sum(centered * centered, axis=0)
            scale = lax.rsqrt(total * (1.0 / 128) + NORM_EPS)[None]
            for cb in range(8):
                sl = slice(cb * 16, (cb + 1) * 16)
                y = (t_ref[sl, grp].astype(F32) - mean) * scale * gout_ref[sl] + bout_ref[sl]
                y_buf[cb * 128:(cb + 1) * 128, :] = y.reshape(128, 128)

        def tile(r, inner):
            zf = z_ref[grp, r].astype(F32)
            if finish:
                x = norm_lanes(zf, gin_ref[...], bin_ref[...]).astype(BF16)
                gate = sigmoid(jnp.dot(x, wg_ref[...], preferred_element_type=F32))
                y = y_buf[pl.ds(r, 128, stride=SL), :].astype(BF16)
                update = lax.dot_general(y, wo_ref[...], (((0,), (0,)), ((), ())), preferred_element_type=F32)
                znew = (zf + gate * update).astype(BF16)
                zo_ref[grp, r] = znew
                zf = znew.astype(F32)
            if project:
                x = norm_lanes(zf, gnext_ref[...], bnext_ref[...]).astype(BF16)
                q = lax.dot_general(wp_ref[...], x, (((1,), (1,)), ((), ())), preferred_element_type=F32)
                m = mask_ref[grp, pl.ds(r, 1), :]
                base = pl.multiple_of(r * SWAP, 8)
                sa[pl.ds(base, 128), :] = m * sigmoid(q[128:256]) * q[:128]
                sb[pl.ds(base, 128), :] = m * sigmoid(q[384:]) * q[256:384]
            return inner

        lax.fori_loop(0, SL, tile, 0, unroll=UNROLL)

        if project:
            def swap(cb, inner):
                for u in range(8):
                    c = cb * 8 + u
                    out_a[s, c, grp] = sa[pl.ds(c, SL, stride=SWAP), :].astype(BF16)
                    out_b[s, c, grp] = sb[pl.ds(c, SL, stride=SWAP), :].astype(BF16)
                return inner

            lax.fori_loop(0, 16, swap, 0)

            @pl.when(s == 0)
            def _():
                @pl.when(grp == 0)
                def _():
                    pl.semaphore_wait(pltpu.get_barrier_semaphore(), ND - 1)

                push(grp)
        return carry

    lax.fori_loop(0, 5, group, 0)

    if finish and natural_out:
        def store(r, carry):
            for g in range(GR):
                z_out[g, r, :128] = zo_ref[g, r]
                z_out[g, r, 128:] = zo_ref[GR, r, g * 32:(g + 1) * 32]
            return carry

        lax.fori_loop(0, SL, store, 0)

    if project:
        @pl.when(s > 0)
        def _():
            push(slice(None))

        @pl.when(s == STEPS - 1)
        def _():
            for k, (src, dst) in enumerate(((out_a, a_in), (out_b, b_in))):
                pltpu.make_async_copy(dst, dst, recv_sem.at[k]).wait()
                if project == 'out':
                    sent = src.at[:, pl.ds(0, 128 - 8)]
                elif k == 0:
                    sent = dst.at[pl.ds(0, 15)]
                else:
                    sent = src.at[:, pl.ds(0, 128 - 16)]
                pltpu.make_async_copy(sent, sent, send_sem.at[k]).wait()


def position_call(z, finish_args, project_args, project, collective_id):
    finish, natural_in = finish_args is not None, z.ndim == 4 and z.shape[0] == GR
    full = lambda arr: pl.BlockSpec(arr.shape, lambda s: (0,) * arr.ndim)
    z_spec = pl.BlockSpec((5, SL, 128, 128), lambda s: (0, s, 0, 0))
    n_spec = pl.BlockSpec((GR, SL, B, 128), lambda s: (0, s, 0, 0))
    args, specs = [z], [n_spec if natural_in else z_spec]
    outs, out_specs, scratch = [], [], []
    if natural_in:
        scratch.append(pltpu.VMEM((5, SL, 128, 128), BF16))
    if finish:
        args += list(finish_args)
        specs += [pl.BlockSpec((128, 5, SL, 128), lambda s: (0, 0, s, 0))] + [full(v) for v in finish_args[1:]]
        outs.append(jax.ShapeDtypeStruct((5, RR, 128, 128) if project else (GR, RR, B, 128), BF16))
        out_specs.append(z_spec if project else n_spec)
        scratch.append(pltpu.VMEM((128 * SL, 128), F32))
        if not project:
            scratch.append(pltpu.VMEM((5, SL, 128, 128), BF16))
    if project:
        args += list(project_args)
        specs += [pl.BlockSpec((5, SL, 128), lambda s: (0, s, 0))] + [full(v) for v in project_args[1:]]
        chans = 8 if project == 'out' else 16
        outs += [jax.ShapeDtypeStruct((chans, 4, 5, RR, w), BF16) for w in (512, 512 if project == 'out' else 256)]
        out_specs += [pl.BlockSpec(memory_space=pl.ANY)] * 2
        scratch += [pltpu.VMEM((SWAP * SL, 128), F32)] * 2
        scratch += [pltpu.VMEM((STEPS, 128, 5, SL, 128), BF16)] * 2
        scratch += [pltpu.SemaphoreType.DMA((2,)), pltpu.SemaphoreType.DMA((2,))]
    params = dict(dimension_semantics=('arbitrary',), vmem_limit_bytes=60 * 2 ** 20)
    if project:
        params.update(collective_id=collective_id, has_side_effects=True)
    name = 'position' + ('_finish' if finish else '') + ('_project_' + project if project else '')
    return pl.pallas_call(
        functools.partial(position_kernel, finish, project, natural_in), name=name, grid=(STEPS,),
        in_specs=specs, out_specs=out_specs, out_shape=outs, scratch_shapes=scratch,
        compiler_params=pltpu.CompilerParams(**params))(*args)


def channel_kernel(incoming, a_ref, b_ref, perm_ref, t_in, amat, bmat, tmat, t_out, send_sem, recv_sem):
    c = pl.program_id(0)
    team = 8 if incoming else ND
    each, cols = 128 // team, team // 4
    me = place(team)

    @pl.when(c == 0)
    def _():
        greet(team)

    def rem_columns(ref):
        width = ref.shape[-1]
        packed = ref[0, :, B:, :].astype(F32).reshape(4 * RR, width).astype(BF16)
        return jnp.dot(packed, perm_ref[:width], preferred_element_type=F32)

    def natural(wide, blk):
        return jnp.concatenate([wide[blk * RR:(blk + 1) * RR, g * 128:(g + 1) * 128] for g in range(GR)], axis=0)

    wide = rem_columns(a_ref)
    for blk in range(4):
        amat[blk * B:(blk + 1) * B, :512] = a_ref[0, blk, :B, :]
        amat[blk * B:(blk + 1) * B, 512:] = natural(wide, blk).astype(BF16)
    wide = rem_columns(b_ref)
    for blk in range(4):
        if incoming:
            bmat[blk * B:(blk + 1) * B, :256] = b_ref[0, blk, :B, :]
            bmat[blk * B:(blk + 1) * B, 256:] = natural(wide, blk).astype(BF16)
        else:
            last = natural(wide, blk).astype(BF16)
            bmat[blk * 128:(blk + 1) * 128, :512] = b_ref[0, blk, :128, :]
            bmat[512 + blk * 32:512 + (blk + 1) * 32, :512] = b_ref[0, blk, 128:B, :]
            bmat[blk * 128:(blk + 1) * 128, 512:] = last[:128]
            bmat[512 + blk * 32:512 + (blk + 1) * 32, 512:] = last[128:]
    contract = 0 if incoming else 1
    tmat[...] = lax.dot_general(amat[...], bmat[...], (((contract,), (contract,)), ((), ())), preferred_element_type=F32)

    def rows_of(blk, lanes):
        if incoming:
            return jnp.concatenate([tmat[blk * 128:(blk + 1) * 128, lanes], tmat[512 + blk * 32:512 + (blk + 1) * 32, lanes]], axis=0)
        return tmat[blk * B:(blk + 1) * B, lanes]

    packed = []
    for blk in range(4):
        for j in range(cols):
            t_out[c, blk * cols + j, :B, :] = rows_of(blk, slice(j * 128, (j + 1) * 128)).astype(BF16)
        rem = rows_of(blk, slice(cols * 128, cols * 128 + 128))
        packed.append(jnp.concatenate([rem[g * RR:(g + 1) * RR] for g in range(GR)], axis=1))
    wide = jnp.dot(jnp.concatenate(packed, axis=0).astype(BF16), perm_ref[:, :cols * 128], preferred_element_type=F32)
    for blk in range(4):
        for j in range(cols):
            t_out[c, blk * cols + j, B:, :] = wide[blk * RR:(blk + 1) * RR, j * 128:(j + 1) * 128].astype(BF16)

    @pl.when(c == 0)
    def _():
        pl.semaphore_wait(pltpu.get_barrier_semaphore(), team - 1)

    def send(n, carry):
        other, device = partner(team, n)
        pltpu.make_async_remote_copy(
            src_ref=t_out.at[c, other], dst_ref=t_in.at[me * each + c],
            send_sem=send_sem, recv_sem=recv_sem, device_id=device, device_id_type=MESH).start()
        return carry

    lax.fori_loop(1, team, send, 0)
    pltpu.make_async_copy(t_out.at[c, me], t_in.at[me * each + c], recv_sem).start()

    @pl.when(c == each - 1)
    def _():
        pltpu.make_async_copy(t_in, t_in, recv_sem).wait()
        sent = t_out.at[:, pl.ds(0, team - 1)]
        pltpu.make_async_copy(sent, sent, send_sem).wait()


def channel_call(a_in, b_in, perm, incoming):
    team = 8 if incoming else ND
    each, width = 128 // team, 128 * team // 4
    merge = lambda v: v.reshape(each, 4, 200, v.shape[-1])
    spec = lambda v: pl.BlockSpec((1, 4, 200, v.shape[-1]), lambda c: (c, 0, 0, 0))
    return pl.pallas_call(
        functools.partial(channel_kernel, incoming), name='channel_in' if incoming else 'channel_out', grid=(each,),
        in_specs=[spec(a_in), spec(b_in), pl.BlockSpec((512, 512), lambda c: (0, 0))],
        out_specs=pl.BlockSpec(memory_space=pl.ANY),
        out_shape=jax.ShapeDtypeStruct((128, 200, 128), BF16),
        scratch_shapes=[
            pltpu.VMEM((640, 640), BF16), pltpu.VMEM((640, width + 128), BF16), pltpu.VMEM((640, width + 128), F32),
            pltpu.VMEM((each, team, 200, 128), BF16),
            pltpu.SemaphoreType.DMA, pltpu.SemaphoreType.DMA],
        compiler_params=pltpu.CompilerParams(
            dimension_semantics=('arbitrary',), vmem_limit_bytes=60 * 2 ** 20,
            collective_id=4 if incoming else 3, has_side_effects=True),
    )(merge(a_in), merge(b_in), perm)


def solution(mesh):
    pair_spec = P(('data', 'dap'), 'dap2', None)
    mask_spec = P(('data', 'dap'), 'dap2')

    def local_fn(pair_act, pair_mask, in_gamma, in_beta, w_proj, w_gate, out_gamma, out_beta, w_out):
        mask = to_tiles(pair_mask.astype(F32))
        z = pair_act.reshape(GR, RR, B, 128)
        src = jnp.arange(512)
        perm = (((src % 128) // 32 * 128 + src // 128 * 32 + src % 32)[:, None] == jnp.arange(512)[None, :]).astype(BF16)
        updates = [(layer, u) for layer in range(in_gamma.shape[0]) for u in range(2)]

        def project_args(at):
            return (mask, in_gamma[at][None], in_beta[at][None], w_proj[at].T)

        def finish_args(at, t):
            wide = lambda v: jnp.broadcast_to(v[at][:, None, None], (128, 1, 128))
            return (t.reshape(128, 5, RR, 128), in_gamma[at][None], in_beta[at][None], w_gate[at], wide(out_gamma), wide(out_beta), w_out[at])

        kind = lambda at: 'in' if at[1] else 'out'
        a_in, b_in = position_call(z, None, project_args(updates[0]), 'out', 1)
        for n, at in enumerate(updates):
            t = channel_call(a_in, b_in, perm, at[1] == 1)
            if n + 1 < len(updates):
                after = updates[n + 1]
                ident = 2 if n == 0 else 5 if at[1] else 6
                z, a_in, b_in = position_call(z, finish_args(at, t), project_args(after), kind(after), ident)
            else:
                z, = position_call(z, finish_args(at, t), None, None, None)
        return z.reshape(B, B, 128)

    return jax.shard_map(local_fn, mesh=mesh, in_specs=(pair_spec, mask_spec) + (P(),) * 7, out_specs=pair_spec, check_vma=False)
```

time: 1880 us -> 1670 us (0.89)
  Pallas kernels: 1840 us -> 1640 us
    pallas_call x4, Pallas kernels: 608 us -> 450 us  [channel_call(): pl.pallas_call(functools.partial(channel_kernel, incoming), name='channel...]
    pallas_call x5, Pallas kernels: 1240 us -> 1190 us  [position_call(): pl.pallas_call(functools.partial(position_kernel, finish, project, natura...]
where the time goes in v2:
time: 1670 us; the launch traced here: 1660 us
  Pallas kernels  1640 us (98%)
    pallas_call x5, Pallas kernels, position_call(): pl.pallas_call(functools.partial(position_kernel, finish, project, natura...  1190 us
    pallas_call x4, Pallas kernels, channel_call(): pl.pallas_call(functools.partial(channel_kernel, incoming), name='channel...  450 us

profile of v2, /device:TPU:0, one launch (start us, length us, event | category | flops | bytes accessed | tf_op | source)
XLA Modules:
  0.0 1658.7 jit_solution(3873328937069279911)
XLA Ops:
  0.0 1.4 slice_bitcast_fusion.11
  1.4 0.9 convert_element_type.12
  2.4 0.1 reshape.120
  2.5 0.7 pad_maximum_fusion.refs_1_.refs_8_
  3.2 1.1 fusion.19
  4.3 0.8 copy.20
  5.1 287.7 %position_project_out.1 = (bf16[8,4,5,40,512]{4,3,2,1,0:T(8,128)(2,1)}, bf16[8,4,5,40,512]{4,3,2,1,0:T(8,128)(2,1)}) custom-call(bf16[4,40,160,128]{3,2,1,0:T(8,128)(2,1)} %bitcast.77, f32[5,40,128]{2,1,0:T(8,128)} %pad_maximum_fusion.refs_1_.refs_8_, f32[1,128]{1,0:T(1,128)} %get-tuple-element.56.refs_2_, f32[1,128]{1,0:T(1,128)} %get-tuple-element.49.refs_3_, ...), custom_call_target="tpu_custom_call" | custom-call | tf_op jit(solution)/shard_map/position_project_out/pallas_call | solution.py:242
  292.8 0.9 fusion.perm_ref
  293.7 0.0 copy-start
  293.7 0.0 copy-start.1
  293.7 0.0 copy-start.2
  293.7 0.0 copy-start.3
  293.7 148.1 %channel_out.2 = bf16[128,200,128]{2,1,0:T(8,128)(2,1)} custom-call(bf16[8,4,200,512]{3,2,1,0:T(8,128)(2,1)} %bitcast.89, bf16[8,4,200,512]{3,2,1,0:T(8,128)(2,1)} %bitcast.90, bf16[512,512]{1,0:T(8,128)(2,1)} %fusion.perm_ref), custom_call_target="tpu_custom_call" | custom-call | tf_op jit(solution)/shard_map/channel_out/pallas_call | solution.py:326
  441.8 0.0 copy-done
  441.9 0.0 copy-done.1
  441.9 0.7 slice_bitcast_fusion.1
  442.6 0.8 copy.21
  443.3 0.0 copy-done.2
  443.3 0.8 broadcast_in_dim.59.refs_5_
  444.2 0.0 copy-done.3
  444.2 0.8 broadcast_in_dim.61.refs_6_
  445.0 290.8 %position_finish_project_in.2 = (bf16[5,40,128,128]{3,2,1,0:T(8,128)(2,1)}, bf16[16,4,5,40,512]{4,3,2,1,0:T(8,128)(2,1)}, bf16[16,4,5,40,256]{4,3,2,1,0:T(8,128)(2,1)}) custom-call(bf16[4,40,160,128]{3,2,1,0:T(8,128)(2,1)} %bitcast.78, bf16[128,5,40,128]{3,2,1,0:T(8,128)(2,1)} %bitcast.79, f32[1,128]{1,0:T(1,128)} %get-tuple-element.56.refs_2_, ...), custom_call_target="tpu_custom_call" | custom-call | tf_op jit(solution)/shard_map/position_finish_project_in/pallas_call | solution.py:242
  735.8 76.0 %channel_in.2 = bf16[128,200,128]{2,1,0:T(8,128)(2,1)} custom-call(bf16[16,4,200,512]{3,2,1,0:T(8,128)(2,1)} %bitcast.84, bf16[16,4,200,256]{3,2,1,0:T(8,128)(2,1)} %bitcast.88, bf16[512,512]{1,0:T(8,128)(2,1)} %fusion.perm_ref), custom_call_target="tpu_custom_call" | custom-call | tf_op jit(solution)/shard_map/channel_in/pallas_call | solution.py:326
  811.8 0.8 copy.22
  812.6 0.8 broadcast_in_dim.63.refs_5_
  813.4 0.8 broadcast_in_dim.65.refs_6_
  814.3 290.9 %position_finish_project_out.1 = (bf16[5,40,128,128]{3,2,1,0:T(8,128)(2,1)}, bf16[8,4,5,40,512]{4,3,2,1,0:T(8,128)(2,1)}, bf16[8,4,5,40,512]{4,3,2,1,0:T(8,128)(2,1)}) custom-call(bf16[5,40,128,128]{3,2,1,0:T(8,128)(2,1)} %get-tuple-element.18.refs_0_, bf16[128,5,40,128]{3,2,1,0:T(8,128)(2,1)} %bitcast.81, f32[1,128]{1,0:T(1,128)} %get-tuple-element.57.refs_9_.refs_2_, ...), custom_call_target="tpu_custom_call" | custom-call | tf_op jit(solution)/shard_map/position_finish_project_out/pallas_call | solution.py:242
  1105.2 146.1 %channel_out.3 = bf16[128,200,128]{2,1,0:T(8,128)(2,1)} custom-call(bf16[8,4,200,512]{3,2,1,0:T(8,128)(2,1)} %bitcast.86, bf16[8,4,200,512]{3,2,1,0:T(8,128)(2,1)} %bitcast.87, bf16[512,512]{1,0:T(8,128)(2,1)} %fusion.perm_ref), custom_call_target="tpu_custom_call" | custom-call | tf_op jit(solution)/shard_map/channel_out/pallas_call | solution.py:326
  1251.3 0.8 copy.23
  1252.1 0.8 broadcast_in_dim.67.refs_5_
  1252.9 0.8 broadcast_in_dim.69.refs_6_
  1253.7 289.1 %position_finish_project_in.3 = (bf16[5,40,128,128]{3,2,1,0:T(8,128)(2,1)}, bf16[16,4,5,40,512]{4,3,2,1,0:T(8,128)(2,1)}, bf16[16,4,5,40,256]{4,3,2,1,0:T(8,128)(2,1)}) custom-call(bf16[5,40,128,128]{3,2,1,0:T(8,128)(2,1)} %get-tuple-element.21.refs_0_, bf16[128,5,40,128]{3,2,1,0:T(8,128)(2,1)} %bitcast.80, f32[1,128]{1,0:T(1,128)} %get-tuple-element.55.refs_9_.refs_2_, ...), custom_call_target="tpu_custom_call" | custom-call | tf_op jit(solution)/shard_map/position_finish_project_in/pallas_call | solution.py:242
  1542.7 79.8 %channel_in.3 = bf16[128,200,128]{2,1,0:T(8,128)(2,1)} custom-call(bf16[16,4,200,512]{3,2,1,0:T(8,128)(2,1)} %bitcast.83, bf16[16,4,200,256]{3,2,1,0:T(8,128)(2,1)} %bitcast.85, bf16[512,512]{1,0:T(8,128)(2,1)} %fusion.perm_ref), custom_call_target="tpu_custom_call" | custom-call | tf_op jit(solution)/shard_map/channel_in/pallas_call | solution.py:326
  1622.5 0.8 broadcast_in_dim.71.refs_5_
  1623.4 0.8 broadcast_in_dim.73.refs_6_
  1624.2 34.5 %position_finish.1 = bf16[4,40,160,128]{3,2,1,0:T(8,128)(2,1)} custom-call(bf16[5,40,128,128]{3,2,1,0:T(8,128)(2,1)} %get-tuple-element.24.refs_0_, bf16[128,5,40,128]{3,2,1,0:T(8,128)(2,1)} %bitcast.82, f32[1,128]{1,0:T(1,128)} %get-tuple-element.58.refs_9_.refs_2_, f32[1,128]{1,0:T(1,128)} %get-tuple-element.47.refs_10_.refs_3_, ...), custom_call_target="tpu_custom_call" | custom-call | tf_op jit(solution)/shard_map/position_finish/pallas_call | solution.py:242
  (6 shorter events, 0.1 us)
Async XLA Ops:
  293.7 148.1 %copy-start = (bf16[2,2,128,128]{3,2,1,0:T(8,128)(2,1)S(1)}, bf16[2,2,128,128]{3,2,1,0:T(8,128)(2,1)}, u32[]{:S(2)}) copy-start(bf16[2,2,128,128]{3,2,1,0:T(8,128)(2,1)} %param.17) | copy-start | bytes 393220
  293.7 148.1 %copy-start.1 = (bf16[2,2,128,128]{3,2,1,0:T(8,128)(2,1)S(1)}, bf16[2,2,128,128]{3,2,1,0:T(8,128)(2,1)}, u32[]{:S(2)}) copy-start(bf16[2,2,128,128]{3,2,1,0:T(8,128)(2,1)} %param.14) | copy-start | bytes 393220
  293.7 149.6 %copy-start.2 = (f32[2,2,128]{2,1,0:T(2,128)S(1)}, f32[2,2,128]{2,1,0:T(2,128)}, u32[]{:S(2)}) copy-start(f32[2,2,128]{2,1,0:T(2,128)} %param.15) | copy-start | bytes 6148
  293.7 150.4 %copy-start.3 = (f32[2,2,128]{2,1,0:T(2,128)S(1)}, f32[2,2,128]{2,1,0:T(2,128)}, u32[]{:S(2)}) copy-start(f32[2,2,128]{2,1,0:T(2,128)} %param.16) | copy-start | bytes 6148

commit v3 on v2

v3 whole, which is shorter than its diff:
```python
import functools

import jax
import jax.numpy as jnp
from jax import lax
from jax.experimental import pallas as pl
from jax.experimental.pallas import tpu as pltpu
from jax.sharding import PartitionSpec as P

NORM_EPS = 1e-5
F32 = jnp.float32
BF16 = jnp.bfloat16
MESH = pl.DeviceIdType.MESH
ND = 16
B = 160
GR = 4
RR = 40
SL = 8
STEPS = RR // SL
UNROLL = 4
SWAP = 136


def to_tiles(block):
    rest = block.shape[2:]
    grouped = block.reshape((GR, RR, B) + rest)
    main = grouped[:, :, :128]
    rem = jnp.swapaxes(grouped[:, :, 128:], 0, 1).reshape((1, RR, 128) + rest)
    return jnp.concatenate([main, rem], axis=0)


def sigmoid(v):
    return 0.5 * jnp.tanh(0.5 * v) + 0.5


def norm_lanes(values, gamma, beta):
    centered = values - jnp.mean(values, axis=-1, keepdims=True)
    variance = jnp.mean(centered * centered, axis=-1, keepdims=True)
    return centered * lax.rsqrt(variance + NORM_EPS) * gamma + beta


def place(team):
    row, col = lax.axis_index('dap'), lax.axis_index('dap2')
    return row * 4 + col if team == ND else row * 2 + lax.rem(col, 2)


def partner(team, n):
    other = lax.rem(place(team) + n, team)
    if team == ND:
        return other, {'dap': other // 4, 'dap2': lax.rem(other, 4)}
    half = lax.axis_index('dap2') // 2
    return other, {'dap': other // 2, 'dap2': half * 2 + lax.rem(other, 2)}


def greet(team):
    barrier = pltpu.get_barrier_semaphore()

    def signal(n, carry):
        _, device = partner(team, n)
        pl.semaphore_signal(barrier, inc=1, device_id=device, device_id_type=MESH)
        return carry

    lax.fori_loop(1, team, signal, 0)


class Refs:
    pass


def position_step(finish, project, natural_in, s, r):
    natural_out = not project
    z_ref = r.z_own if natural_in else r.z_in
    if finish:
        zo_ref = r.zo_own if natural_out else r.z_out
    if project:
        row, col = lax.axis_index('dap'), lax.axis_index('dap2')
        rows = pl.ds(pl.multiple_of(s * SL, SL), SL)
        pairs = ((r.out_a, r.a_in), (r.out_b, r.b_in))

        def push(grp):
            for k, (src, dst) in enumerate(pairs):
                team = 8 if project == 'in' and k == 1 else ND
                split = 8 if project == 'in' else ND
                each = 128 // split
                lane = col if team == ND else lax.rem(col, 2)
                lanes = pl.ds(pl.multiple_of(lane * 128, 128), 128)
                there = dst.at[:, row, grp, rows, lanes]

                def part(index):
                    return src.at[s, pl.ds(index * each, each), grp]

                def send(n, carry):
                    other, device = partner(team, n)
                    if team != split:
                        other = device['dap'] * 2 + lax.rem(device['dap2'], 2)
                    pltpu.make_async_remote_copy(
                        src_ref=part(other), dst_ref=there, send_sem=r.send_sem.at[k], recv_sem=r.recv_sem.at[k],
                        device_id=device, device_id_type=MESH).start()
                    return carry

                lax.fori_loop(1, team, send, 0)
                pltpu.make_async_copy(part(place(split)), there, r.recv_sem.at[k]).start()

    if natural_in:
        def load(n, carry):
            for g in range(GR):
                z_ref[g, n] = r.z_in[g, n, :128]
                z_ref[GR, n, g * 32:(g + 1) * 32] = r.z_in[g, n, 128:]
            return carry

        lax.fori_loop(0, SL, load, 0)

    def group(grp, carry):
        if finish:
            total = jnp.zeros((SL, 128), F32)
            for cb in range(8):
                total += jnp.sum(r.tri(cb * 16, grp).astype(F32), axis=0)
            mean = (total * (1.0 / 128))[None]
            total = jnp.zeros((SL, 128), F32)
            for cb in range(8):
                centered = r.tri(cb * 16, grp).astype(F32) - mean
                total += jnp.sum(centered * centered, axis=0)
            scale = lax.rsqrt(total * (1.0 / 128) + NORM_EPS)[None]
            for cb in range(8):
                sl = slice(cb * 16, (cb + 1) * 16)
                y = (r.tri(cb * 16, grp).astype(F32) - mean) * scale * r.gout[0, 0, sl] + r.bout[0, 0, sl]
                r.y_buf[cb * 128:(cb + 1) * 128, :] = y.reshape(128, 128)

        def tile(n, inner):
            zf = z_ref[grp, n].astype(F32)
            if finish:
                x = norm_lanes(zf, r.gin[0, 0], r.bin[0, 0]).astype(BF16)
                gate = sigmoid(jnp.dot(x, r.wg[0, 0], preferred_element_type=F32))
                y = r.y_buf[pl.ds(n, 128, stride=SL), :].astype(BF16)
                update = lax.dot_general(y, r.wo[0, 0], (((0,), (0,)), ((), ())), preferred_element_type=F32)
                znew = (zf + gate * update).astype(BF16)
                zo_ref[grp, n] = znew
                zf = znew.astype(F32)
            if project:
                x = norm_lanes(zf, r.gnext[0, 0], r.bnext[0, 0]).astype(BF16)
                q = lax.dot_general(r.wp[0, 0], x, (((1,), (1,)), ((), ())), preferred_element_type=F32)
                m = r.mask[grp, pl.ds(n, 1), :]
                base = pl.multiple_of(n * SWAP, 8)
                r.sa[pl.ds(base, 128), :] = m * sigmoid(q[128:256]) * q[:128]
                r.sb[pl.ds(base, 128), :] = m * sigmoid(q[384:]) * q[256:384]
            return inner

        lax.fori_loop(0, SL, tile, 0, unroll=UNROLL)

        if project:
            def swap(cb, inner):
                for u in range(8):
                    c = cb * 8 + u
                    r.out_a[s, c, grp] = r.sa[pl.ds(c, SL, stride=SWAP), :].astype(BF16)
                    r.out_b[s, c, grp] = r.sb[pl.ds(c, SL, stride=SWAP), :].astype(BF16)
                return inner

            lax.fori_loop(0, 16, swap, 0)

            @pl.when(s == 0)
            def _():
                if not r.greeted:
                    @pl.when(grp == 0)
                    def _():
                        pl.semaphore_wait(pltpu.get_barrier_semaphore(), ND - 1)

                push(grp)
        return carry

    lax.fori_loop(0, 5, group, 0)

    if finish and natural_out:
        def store(n, carry):
            for g in range(GR):
                r.z_out[g, n, :128] = zo_ref[g, n]
                r.z_out[g, n, 128:] = zo_ref[GR, n, g * 32:(g + 1) * 32]
            return carry

        lax.fori_loop(0, SL, store, 0)

    if project:
        @pl.when(s > 0)
        def _():
            push(slice(None))

        @pl.when(s == STEPS - 1)
        def _():
            for k, (src, dst) in enumerate(pairs):
                pltpu.make_async_copy(dst, dst, r.recv_sem.at[k]).wait()
                if project == 'out':
                    sent = src.at[:, pl.ds(0, 128 - 8)]
                elif k == 0:
                    sent = dst.at[pl.ds(0, 15)]
                else:
                    sent = src.at[:, pl.ds(0, 128 - 16)]
                pltpu.make_async_copy(sent, sent, r.send_sem.at[k]).wait()


def channel_step(incoming, r, put_main, put_rem):
    cols = 2 if incoming else 4

    def rem_columns(ref):
        width = ref.shape[-1]
        packed = ref[0, :, B:, :].astype(F32).reshape(4 * RR, width).astype(BF16)
        return jnp.dot(packed, r.perm[:width], preferred_element_type=F32)

    def natural(wide, blk):
        return jnp.concatenate([wide[blk * RR:(blk + 1) * RR, g * 128:(g + 1) * 128] for g in range(GR)], axis=0)

    wide = rem_columns(r.a)
    for blk in range(4):
        r.amat[blk * B:(blk + 1) * B, :512] = r.a[0, blk, :B, :]
        r.amat[blk * B:(blk + 1) * B, 512:] = natural(wide, blk).astype(BF16)
    wide = rem_columns(r.b)
    for blk in range(4):
        last = natural(wide, blk).astype(BF16)
        if incoming:
            r.bmat[blk * B:(blk + 1) * B, :256] = r.b[0, blk, :B, :]
            r.bmat[blk * B:(blk + 1) * B, 256:] = last
        else:
            r.bmat[blk * 128:(blk + 1) * 128, :512] = r.b[0, blk, :128, :]
            r.bmat[512 + blk * 32:512 + (blk + 1) * 32, :512] = r.b[0, blk, 128:B, :]
            r.bmat[blk * 128:(blk + 1) * 128, 512:] = last[:128]
            r.bmat[512 + blk * 32:512 + (blk + 1) * 32, 512:] = last[128:]
    contract = 0 if incoming else 1
    r.tmat[...] = lax.dot_general(r.amat[...], r.bmat[...], (((contract,), (contract,)), ((), ())), preferred_element_type=F32)

    def rows_of(blk, lanes):
        if incoming:
            return jnp.concatenate([r.tmat[blk * 128:(blk + 1) * 128, lanes], r.tmat[512 + blk * 32:512 + (blk + 1) * 32, lanes]], axis=0)
        return r.tmat[blk * B:(blk + 1) * B, lanes]

    packed = []
    for blk in range(4):
        for j in range(cols):
            put_main(blk * cols + j, rows_of(blk, slice(j * 128, (j + 1) * 128)))
        rem = rows_of(blk, slice(cols * 128, cols * 128 + 128))
        packed.append(jnp.concatenate([rem[g * RR:(g + 1) * RR] for g in range(GR)], axis=1))
    wide = jnp.dot(jnp.concatenate(packed, axis=0).astype(BF16), r.perm[:, :cols * 128], preferred_element_type=F32)
    for blk in range(4):
        for j in range(cols):
            put_rem(blk * cols + j, wide[blk * RR:(blk + 1) * RR, j * 128:(j + 1) * 128])


def channel_out_kernel(a_ref, b_ref, perm_ref, t_in, amat, bmat, tmat, t_out, send_sem, recv_sem):
    r = Refs()
    r.a, r.b, r.perm, r.amat, r.bmat, r.tmat = a_ref, b_ref, perm_ref, amat, bmat, tmat
    c = pl.program_id(0)
    me = place(ND)

    @pl.when(c == 0)
    def _():
        greet(ND)

    def put_main(owner, v):
        t_out[c, owner, :B, :] = v.astype(BF16)

    def put_rem(owner, v):
        t_out[c, owner, B:, :] = v.astype(BF16)

    channel_step(False, r, put_main, put_rem)

    @pl.when(c == 0)
    def _():
        pl.semaphore_wait(pltpu.get_barrier_semaphore(), ND - 1)

    def send(n, carry):
        other, device = partner(ND, n)
        pltpu.make_async_remote_copy(
            src_ref=t_out.at[c, other], dst_ref=t_in.at[me * 8 + c],
            send_sem=send_sem, recv_sem=recv_sem, device_id=device, device_id_type=MESH).start()
        return carry

    lax.fori_loop(1, ND, send, 0)
    pltpu.make_async_copy(t_out.at[c, me], t_in.at[me * 8 + c], recv_sem).start()

    @pl.when(c == 7)
    def _():
        pltpu.make_async_copy(t_in, t_in, recv_sem).wait()
        sent = t_out.at[:, pl.ds(0, ND - 1)]
        pltpu.make_async_copy(sent, sent, send_sem).wait()


def fused_kernel(channels, finish, project, natural_in, *refs):
    refs = list(refs)
    take = lambda: refs.pop(0)
    r = Refs()
    if channels:
        r.a, r.b, r.perm = take(), take(), take()
    r.z_in = take()
    if finish:
        if not channels:
            t_ref = take()
            r.tri = lambda c0, grp: t_ref[c0:c0 + 16, grp]
        r.gin, r.bin, r.wg, r.gout, r.bout, r.wo = [take() for _ in range(6)]
    if project:
        r.mask, r.gnext, r.bnext, r.wp = [take() for _ in range(4)]
    if finish:
        r.z_out = take()
    if project:
        r.a_in, r.b_in = take(), take()
    if natural_in:
        r.z_own = take()
    if finish:
        r.y_buf = take()
        if not project:
            r.zo_own = take()
    if project:
        r.sa, r.sb, r.out_a, r.out_b, r.send_sem, r.recv_sem = [take() for _ in range(6)]
    step = pl.program_id(0)
    team = ND if project else 8
    if project or channels:
        @pl.when(step == 0)
        def _():
            greet(team)
    r.greeted = channels
    if not channels:
        position_step(finish, project, natural_in, step, r)
        return
    r.amat, r.bmat, r.tmat, t_out, t_own, send_t, recv_t = [take() for _ in range(7)]
    me = place(8)

    @pl.when(step < 16)
    def _():
        def put_main(owner, v):
            tiles = v.reshape(GR, STEPS, SL, 128).astype(BF16)
            for s in range(STEPS):
                t_out[step, owner, s, :GR] = tiles[:, s]

        def put_rem(owner, v):
            t_out[step, owner, :, GR] = v.reshape(STEPS, SL, 128).astype(BF16)

        channel_step(True, r, put_main, put_rem)
        t_own[me * 16 + step] = t_out[step, me]

    @pl.when(step == 15)
    def _():
        pl.semaphore_wait(pltpu.get_barrier_semaphore(), team - 1)

        def slab(s, carry):
            def send(n, inner):
                other, device = partner(8, n)
                pltpu.make_async_remote_copy(
                    src_ref=t_out.at[:, other, s], dst_ref=t_own.at[pl.ds(me * 16, 16), s],
                    send_sem=send_t, recv_sem=recv_t.at[s], device_id=device, device_id_type=MESH).start()
                return inner

            return lax.fori_loop(1, 8, send, carry)

        lax.fori_loop(0, STEPS, slab, 0)

    @pl.when(step >= 16)
    def _():
        s = step - 16
        landed = t_own.at[pl.ds(0, 112), s]
        pltpu.make_async_copy(landed, landed, recv_t.at[s]).wait()
        r.tri = lambda c0, grp: t_own[c0:c0 + 16, s, grp]
        position_step(finish, project, natural_in, s, r)

    @pl.when(step == 16 + STEPS - 1)
    def _():
        sent = t_out.at[:, pl.ds(0, 7)]
        pltpu.make_async_copy(sent, sent, send_t).wait()


def fused_call(z, at, t, params, after, channels, collective_id):
    finish, project = at is not None, None if after is None else 'in' if after[1] else 'out'
    natural_in = z.shape[0] == GR
    first = 16 if channels else 0
    slab = lambda n: jnp.maximum(n - first, 0) if channels else n
    z_spec = pl.BlockSpec((5, SL, 128, 128), lambda n: (0, slab(n), 0, 0))
    n_spec = pl.BlockSpec((GR, SL, B, 128), lambda n: (0, slab(n), 0, 0))

    def weight(name, which):
        arr = params[name]
        return arr, pl.BlockSpec((1, 1) + arr.shape[2:], lambda n: tuple(which) + (0,) * (arr.ndim - 2))

    ins, outs, scratch = [], [], []
    if channels:
        a_in, b_in, perm = t
        for v in (a_in, b_in):
            v = v.reshape(16, 4, 200, v.shape[-1])
            ins.append((v, pl.BlockSpec((1,) + v.shape[1:], lambda n: (jnp.minimum(n, 15), 0, 0, 0))))
        ins.append((perm, pl.BlockSpec((512, 512), lambda n: (0, 0))))
    ins.append((z, n_spec if natural_in else z_spec))
    if natural_in:
        scratch.append(pltpu.VMEM((5, SL, 128, 128), BF16))
    if finish:
        if not channels:
            ins.append((t.reshape(128, 5, RR, 128), pl.BlockSpec((128, 5, SL, 128), lambda n: (0, 0, n, 0))))
        ins += [weight(name, at) for name in ('gin', 'bin', 'wg', 'gout', 'bout', 'wo')]
        outs.append((jax.ShapeDtypeStruct((5, RR, 128, 128) if project else (GR, RR, B, 128), BF16), z_spec if project else n_spec))
        scratch.append(pltpu.VMEM((128 * SL, 128), F32))
        if not project:
            scratch.append(pltpu.VMEM((5, SL, 128, 128), BF16))
    if project:
        ins.append((params['mask'], pl.BlockSpec((5, SL, 128), lambda n: (0, slab(n), 0))))
        ins += [weight(name, after) for name in ('gin', 'bin', 'wp')]
        chans = 8 if project == 'out' else 16
        anywhere = pl.BlockSpec(memory_space=pl.ANY)
        outs += [(jax.ShapeDtypeStruct((chans, 4, 5, RR, w), BF16), anywhere) for w in (512, 512 if project == 'out' else 256)]
        scratch += [pltpu.VMEM((SWAP * SL, 128), F32)] * 2
        scratch += [pltpu.VMEM((STEPS, 128, 5, SL, 128), BF16)] * 2
        scratch += [pltpu.SemaphoreType.DMA((2,)), pltpu.SemaphoreType.DMA((2,))]
    if channels:
        scratch += [pltpu.VMEM((640, 640), BF16), pltpu.VMEM((640, 384), BF16), pltpu.VMEM((640, 384), F32)]
        scratch += [pltpu.VMEM((16, 8, STEPS, 5, SL, 128), BF16), pltpu.VMEM((128, STEPS, 5, SL, 128), BF16)]
        scratch += [pltpu.SemaphoreType.DMA, pltpu.SemaphoreType.DMA((STEPS,))]
    extra = dict(dimension_semantics=('arbitrary',), vmem_limit_bytes=60 * 2 ** 20)
    if project or channels:
        extra.update(collective_id=collective_id, has_side_effects=True)
    name = '_'.join((['channels'] if channels else []) + (['finish'] if finish else []) + (['project', project] if project else []))
    return pl.pallas_call(
        functools.partial(fused_kernel, channels, finish, project, natural_in), name=name, grid=(first + STEPS,),
        in_specs=[spec for _, spec in ins], out_specs=[spec for _, spec in outs], out_shape=[shape for shape, _ in outs],
        scratch_shapes=scratch, compiler_params=pltpu.CompilerParams(**extra))(*[v for v, _ in ins])


def channel_call(a_in, b_in, perm):
    merge = lambda v: v.reshape(8, 4, 200, 512)
    spec = pl.BlockSpec((1, 4, 200, 512), lambda c: (c, 0, 0, 0))
    return pl.pallas_call(
        channel_out_kernel, name='channels_out', grid=(8,),
        in_specs=[spec, spec, pl.BlockSpec((512, 512), lambda c: (0, 0))],
        out_specs=pl.BlockSpec(memory_space=pl.ANY),
        out_shape=jax.ShapeDtypeStruct((128, 200, 128), BF16),
        scratch_shapes=[
            pltpu.VMEM((640, 640), BF16), pltpu.VMEM((640, 640), BF16), pltpu.VMEM((640, 640), F32),
            pltpu.VMEM((8, ND, 200, 128), BF16),
            pltpu.SemaphoreType.DMA, pltpu.SemaphoreType.DMA],
        compiler_params=pltpu.CompilerParams(
            dimension_semantics=('arbitrary',), vmem_limit_bytes=60 * 2 ** 20, collective_id=3, has_side_effects=True),
    )(merge(a_in), merge(b_in), perm)


def solution(mesh):
    pair_spec = P(('data', 'dap'), 'dap2', None)
    mask_spec = P(('data', 'dap'), 'dap2')

    def local_fn(pair_act, pair_mask, in_gamma, in_beta, w_proj, w_gate, out_gamma, out_beta, w_out):
        mask = to_tiles(pair_mask.astype(F32))
        z = pair_act.reshape(GR, RR, B, 128)
        src = jnp.arange(512)
        perm = (((src % 128) // 32 * 128 + src // 128 * 32 + src % 32)[:, None] == jnp.arange(512)[None, :]).astype(BF16)
        rowed = lambda v: v[:, :, None, :]
        wide = lambda v: jnp.broadcast_to(v[..., None, None], v.shape + (1, 128))
        params = dict(
            mask=mask, gin=rowed(in_gamma), bin=rowed(in_beta), wp=jnp.swapaxes(w_proj, 2, 3), wg=w_gate,
            gout=wide(out_gamma), bout=wide(out_beta), wo=w_out)
        layers = in_gamma.shape[0]
        a_in, b_in = fused_call(z, None, None, params, (0, 0), False, 1)
        for layer in range(layers):
            t = channel_call(a_in, b_in, perm)
            z, a_in, b_in = fused_call(z, (layer, 0), t, params, (layer, 1), False, 2 if layer == 0 else 4)
            if layer + 1 < layers:
                z, a_in, b_in = fused_call(z, (layer, 1), (a_in, b_in, perm), params, (layer + 1, 0), True, 5)
            else:
                z, = fused_call(z, (layer, 1), (a_in, b_in, perm), params, None, True, 6)
        return z.reshape(B, B, 128)

    return jax.shard_map(local_fn, mesh=mesh, in_specs=(pair_spec, mask_spec) + (P(),) * 7, out_specs=pair_spec, check_vma=False)
```

time: 1670 us -> 1620 us (0.970)
  Pallas kernels: 1640 us -> 1600 us
    pallas_call x9 -> x7, Pallas kernels: 1640 us -> 1600 us  [the longest x5 1300 us: fused_call(): pl.pallas_call(functools.partial(fused_kernel, channels, finish, project,...]
where the time goes in v3:
time: 1620 us; the launch traced here: 1610 us
  Pallas kernels  1600 us (99%)
    pallas_call x5, Pallas kernels, fused_call(): pl.pallas_call(functools.partial(fused_kernel, channels, finish, project,...  1300 us
    pallas_call x2, Pallas kernels, channel_call(): pl.pallas_call(channel_out_kernel, name='channels_out', grid=(8,), in_spe...  299 us

profile of v3, /device:TPU:0, one launch (start us, length us, event | category | flops | bytes accessed | tf_op | source)
XLA Modules:
  0.0 1611.8 jit_solution(1593923626760100084)
XLA Ops:
  0.0 0.9 convert_element_type.12
  1.0 0.1 reshape.96
  1.1 0.6 pad_maximum_fusion.refs_1_.refs_8_.refs_10_
  1.7 2.0 broadcast_in_dim.10.refs_5_.refs_7_
  3.7 2.0 broadcast_in_dim.11.refs_6_.refs_8_
  5.7 1.0 fusion.perm_ref.refs_2_
  6.7 2.0 copy.13
  8.7 288.2 %project_out.1 = (bf16[8,4,5,40,512]{4,3,2,1,0:T(8,128)(2,1)}, bf16[8,4,5,40,512]{4,3,2,1,0:T(8,128)(2,1)}) custom-call(bf16[4,40,160,128]{3,2,1,0:T(8,128)(2,1)} %bitcast.20, f32[5,40,128]{2,1,0:T(8,128)} %pad_maximum_fusion.refs_1_.refs_8_.refs_10_, f32[2,2,1,128]{3,2,1,0:T(1,128)} %bitcast.37, f32[2,2,1,128]{3,2,1,0:T(1,128)} %bitcast.45, ...), custom_call_target="tpu_custom_call" | custom-call | tf_op jit(solution)/shard_map/project_out/pallas_call | solution.py:413
  297.0 147.8 %channels_out.2 = bf16[128,200,128]{2,1,0:T(8,128)(2,1)} custom-call(bf16[8,4,200,512]{3,2,1,0:T(8,128)(2,1)} %bitcast.32, bf16[8,4,200,512]{3,2,1,0:T(8,128)(2,1)} %bitcast.33, bf16[512,512]{1,0:T(8,128)(2,1)} %fusion.perm_ref.refs_2_), custom_call_target="tpu_custom_call" | custom-call | tf_op jit(solution)/shard_map/channels_out/pallas_call | solution.py:422
  444.8 290.1 %finish_project_in.2 = (bf16[5,40,128,128]{3,2,1,0:T(8,128)(2,1)}, bf16[16,4,5,40,512]{4,3,2,1,0:T(8,128)(2,1)}, bf16[16,4,5,40,256]{4,3,2,1,0:T(8,128)(2,1)}) custom-call(bf16[4,40,160,128]{3,2,1,0:T(8,128)(2,1)} %bitcast.21, bf16[128,5,40,128]{3,2,1,0:T(8,128)(2,1)} %bitcast.19, f32[2,2,1,128]{3,2,1,0:T(1,128)} %bitcast.38, f32[2,2,1,128]{3,2,1,0:T(1,128)} %bitcast.46, ...), custom_call_target="tpu_custom_call" | custom-call | tf_op jit(solution)/shard_map/finish_project_in/pallas_call | solution.py:413
  734.9 326.8 %channels_finish_project_out.1 = (bf16[5,40,128,128]{3,2,1,0:T(8,128)(2,1)}, bf16[8,4,5,40,512]{4,3,2,1,0:T(8,128)(2,1)}, bf16[8,4,5,40,512]{4,3,2,1,0:T(8,128)(2,1)}) custom-call(bf16[16,4,200,512]{3,2,1,0:T(8,128)(2,1)} %bitcast.27, bf16[16,4,200,256]{3,2,1,0:T(8,128)(2,1)} %bitcast.29, bf16[512,512]{1,0:T(8,128)(2,1)} %fusion.perm_ref.refs_2_, ...), custom_call_target="tpu_custom_call" | custom-call | tf_op jit(solution)/shard_map/channels_finish_project_out/pallas_call | solution.py:413
  1061.8 150.7 %channels_out.3 = bf16[128,200,128]{2,1,0:T(8,128)(2,1)} custom-call(bf16[8,4,200,512]{3,2,1,0:T(8,128)(2,1)} %bitcast.30, bf16[8,4,200,512]{3,2,1,0:T(8,128)(2,1)} %bitcast.31, bf16[512,512]{1,0:T(8,128)(2,1)} %fusion.perm_ref.refs_2_), custom_call_target="tpu_custom_call" | custom-call | tf_op jit(solution)/shard_map/channels_out/pallas_call | solution.py:422
  1212.5 291.2 %finish_project_in.3 = (bf16[5,40,128,128]{3,2,1,0:T(8,128)(2,1)}, bf16[16,4,5,40,512]{4,3,2,1,0:T(8,128)(2,1)}, bf16[16,4,5,40,256]{4,3,2,1,0:T(8,128)(2,1)}) custom-call(bf16[5,40,128,128]{3,2,1,0:T(8,128)(2,1)} %get-tuple-element.21.refs_0_, bf16[128,5,40,128]{3,2,1,0:T(8,128)(2,1)} %bitcast.18, f32[2,2,1,128]{3,2,1,0:T(1,128)} %bitcast.42, ...), custom_call_target="tpu_custom_call" | custom-call | tf_op jit(solution)/shard_map/finish_project_in/pallas_call | solution.py:413
  1503.7 101.3 %channels_finish.1 = bf16[4,40,160,128]{3,2,1,0:T(8,128)(2,1)} custom-call(bf16[16,4,200,512]{3,2,1,0:T(8,128)(2,1)} %bitcast.28, bf16[16,4,200,256]{3,2,1,0:T(8,128)(2,1)} %bitcast.34, bf16[512,512]{1,0:T(8,128)(2,1)} %fusion.perm_ref.refs_2_, bf16[5,40,128,128]{3,2,1,0:T(8,128)(2,1)} %get-tuple-element.26.refs_3_, f32[2,2,1,128]{3,2,1,0:T(1,128)} %bitcast.44, ...), custom_call_target="tpu_custom_call" | custom-call | tf_op jit(solution)/shard_map/channels_finish/pallas_call | solution.py:413
  1605.0 6.8 copy.15
  (4 shorter events, 0.0 us)

commit v4 on v3

v4 whole, which is shorter than its diff:
```python
import functools

import jax
import jax.numpy as jnp
from jax import lax
from jax.experimental import pallas as pl
from jax.experimental.pallas import tpu as pltpu
from jax.sharding import PartitionSpec as P

NORM_EPS = 1e-5
F32 = jnp.float32
BF16 = jnp.bfloat16
MESH = pl.DeviceIdType.MESH
ND = 16
B = 160
GR = 4
RR = 40
SL = 8
STEPS = RR // SL
UNROLL = 4
SPLIT = (2, 4, 8, 8)
SWAP = 136


def to_tiles(block):
    rest = block.shape[2:]
    grouped = block.reshape((GR, RR, B) + rest)
    main = grouped[:, :, :128]
    rem = jnp.swapaxes(grouped[:, :, 128:], 0, 1).reshape((1, RR, 128) + rest)
    return jnp.concatenate([main, rem], axis=0)


def sigmoid(v):
    return 0.5 * jnp.tanh(0.5 * v) + 0.5


def norm_lanes(values, gamma, beta):
    centered = values - jnp.mean(values, axis=-1, keepdims=True)
    variance = jnp.mean(centered * centered, axis=-1, keepdims=True)
    return centered * lax.rsqrt(variance + NORM_EPS) * gamma + beta


def place(team):
    row, col = lax.axis_index('dap'), lax.axis_index('dap2')
    return row * 4 + col if team == ND else row * 2 + lax.rem(col, 2)


def partner(team, n):
    other = lax.rem(place(team) + n, team)
    if team == ND:
        return other, {'dap': other // 4, 'dap2': lax.rem(other, 4)}
    half = lax.axis_index('dap2') // 2
    return other, {'dap': other // 2, 'dap2': half * 2 + lax.rem(other, 2)}


def greet(team):
    barrier = pltpu.get_barrier_semaphore()

    def signal(n, carry):
        _, device = partner(team, n)
        pl.semaphore_signal(barrier, inc=1, device_id=device, device_id_type=MESH)
        return carry

    lax.fori_loop(1, team, signal, 0)


class Refs:
    pass


WHOLE = 3


def channel_groups(kind):
    each = 16 if kind == 'in' else 8
    sizes = [each // n for n in SPLIT]
    return tuple((sum(sizes[:n]), sizes[n]) for n in range(len(SPLIT)))


def group_bytes(ref, q):
    if q == 0:
        return ref.at[:, :, pl.ds(0, 4)]
    return ref.at[pl.ds(0, 2 * ref.shape[0] // SPLIT[q]), :, pl.ds(0, 1)]


def position_step(finish, project, natural_in, s, r):
    natural_out = not project
    z_ref = r.z_own if natural_in else r.z_in
    if finish:
        zo_ref = r.zo_own if natural_out else r.z_out
    if project:
        row, col = lax.axis_index('dap'), lax.axis_index('dap2')
        pairs = ((r.out_a, r.a_in), (r.out_b, r.b_in))

        def push(q, slab, grp):
            start, count = (0, 16 if project == 'in' else 8) if q is None else channel_groups(project)[q]
            sem = 0 if q is None else q
            rows = pl.ds(pl.multiple_of(slab * SL, SL), SL)
            for k, (src, dst) in enumerate(pairs):
                team = 8 if project == 'in' and k == 1 else ND
                split = 8 if project == 'in' else ND
                each = 128 // split
                lane = col if team == ND else lax.rem(col, 2)
                lanes = pl.ds(pl.multiple_of(lane * 128, 128), 128)
                there = dst.at[pl.ds(start, count), row, grp, rows, lanes]

                def part(index):
                    return src.at[slab, pl.ds(index * each + start, count), grp]

                def send(n, carry):
                    other, device = partner(team, n)
                    if team != split:
                        other = device['dap'] * 2 + lax.rem(device['dap2'], 2)
                    pltpu.make_async_remote_copy(
                        src_ref=part(other), dst_ref=there, send_sem=r.send_sem.at[k], recv_sem=r.recv_sem.at[k, sem],
                        device_id=device, device_id_type=MESH).start()
                    return carry

                lax.fori_loop(1, team, send, 0)
                pltpu.make_async_copy(part(place(split)), there, r.recv_sem.at[k, sem]).start()

    if natural_in:
        def load(n, carry):
            for g in range(GR):
                z_ref[g, n] = r.z_in[g, n, :128]
                z_ref[GR, n, g * 32:(g + 1) * 32] = r.z_in[g, n, 128:]
            return carry

        lax.fori_loop(0, SL, load, 0)

    def group(grp, carry):
        if finish:
            @pl.when(s == 0)
            def _():
                r.arrive(grp)

            total = jnp.zeros((SL, 128), F32)
            for cb in range(8):
                total += jnp.sum(r.tri(cb * 16, grp).astype(F32), axis=0)
            mean = (total * (1.0 / 128))[None]
            total = jnp.zeros((SL, 128), F32)
            for cb in range(8):
                centered = r.tri(cb * 16, grp).astype(F32) - mean
                total += jnp.sum(centered * centered, axis=0)
            scale = lax.rsqrt(total * (1.0 / 128) + NORM_EPS)[None]
            for cb in range(8):
                sl = slice(cb * 16, (cb + 1) * 16)
                y = (r.tri(cb * 16, grp).astype(F32) - mean) * scale * r.gout[0, 0, sl] + r.bout[0, 0, sl]
                r.y_buf[cb * 128:(cb + 1) * 128, :] = y.reshape(128, 128)

        def tile(n, inner):
            zf = z_ref[grp, n].astype(F32)
            if finish:
                x = norm_lanes(zf, r.gin[0, 0], r.bin[0, 0]).astype(BF16)
                gate = sigmoid(jnp.dot(x, r.wg[0, 0], preferred_element_type=F32))
                y = r.y_buf[pl.ds(n, 128, stride=SL), :].astype(BF16)
                update = lax.dot_general(y, r.wo[0, 0], (((0,), (0,)), ((), ())), preferred_element_type=F32)
                znew = (zf + gate * update).astype(BF16)
                zo_ref[grp, n] = znew
                zf = znew.astype(F32)
            if project:
                x = norm_lanes(zf, r.gnext[0, 0], r.bnext[0, 0]).astype(BF16)
                q = lax.dot_general(r.wp[0, 0], x, (((1,), (1,)), ((), ())), preferred_element_type=F32)
                m = r.mask[grp, pl.ds(n, 1), :]
                base = pl.multiple_of(n * SWAP, 8)
                r.sa[pl.ds(base, 128), :] = m * sigmoid(q[128:256]) * q[:128]
                r.sb[pl.ds(base, 128), :] = m * sigmoid(q[384:]) * q[256:384]
            return inner

        lax.fori_loop(0, SL, tile, 0, unroll=UNROLL)

        if project:
            def swap(cb, inner):
                for u in range(8):
                    c = cb * 8 + u
                    r.out_a[s, c, grp] = r.sa[pl.ds(c, SL, stride=SWAP), :].astype(BF16)
                    r.out_b[s, c, grp] = r.sb[pl.ds(c, SL, stride=SWAP), :].astype(BF16)
                return inner

            lax.fori_loop(0, 16, swap, 0)

            @pl.when(s == 0)
            def _():
                if not finish:
                    @pl.when(grp == 0)
                    def _():
                        pl.semaphore_wait(pltpu.get_barrier_semaphore(), ND - 1)

                push(None, s, grp)
        return carry

    lax.fori_loop(0, 5, group, 0)

    if finish and natural_out:
        def store(n, carry):
            for g in range(GR):
                r.z_out[g, n, :128] = zo_ref[g, n]
                r.z_out[g, n, 128:] = zo_ref[GR, n, g * 32:(g + 1) * 32]
            return carry

        lax.fori_loop(0, SL, store, 0)

    if project:
        @pl.when((s > 0) & (s < WHOLE))
        def _():
            push(None, s, slice(None))

        @pl.when(s >= WHOLE)
        def _():
            push(0, s, slice(None))

        @pl.when(s == STEPS - 1)
        def _():
            for q in range(1, len(channel_groups(project))):
                def later(slab, carry):
                    push(q, slab, slice(None))
                    return carry

                lax.fori_loop(WHOLE, STEPS, later, 0)


def channel_step(incoming, r, put_main, put_rem):
    cols = 2 if incoming else 4

    def rem_columns(ref):
        width = ref.shape[-1]
        packed = ref[0, :, B:, :].astype(F32).reshape(4 * RR, width).astype(BF16)
        return jnp.dot(packed, r.perm[:width], preferred_element_type=F32)

    def natural(wide, blk):
        return jnp.concatenate([wide[blk * RR:(blk + 1) * RR, g * 128:(g + 1) * 128] for g in range(GR)], axis=0)

    wide = rem_columns(r.a)
    for blk in range(4):
        r.amat[blk * B:(blk + 1) * B, :512] = r.a[0, blk, :B, :]
        r.amat[blk * B:(blk + 1) * B, 512:] = natural(wide, blk).astype(BF16)
    wide = rem_columns(r.b)
    for blk in range(4):
        last = natural(wide, blk).astype(BF16)
        if incoming:
            r.bmat[blk * B:(blk + 1) * B, :256] = r.b[0, blk, :B, :]
            r.bmat[blk * B:(blk + 1) * B, 256:] = last
        else:
            r.bmat[blk * 128:(blk + 1) * 128, :512] = r.b[0, blk, :128, :]
            r.bmat[512 + blk * 32:512 + (blk + 1) * 32, :512] = r.b[0, blk, 128:B, :]
            r.bmat[blk * 128:(blk + 1) * 128, 512:] = last[:128]
            r.bmat[512 + blk * 32:512 + (blk + 1) * 32, 512:] = last[128:]
    contract = 0 if incoming else 1
    r.tmat[...] = lax.dot_general(r.amat[...], r.bmat[...], (((contract,), (contract,)), ((), ())), preferred_element_type=F32)

    def rows_of(blk, lanes):
        if incoming:
            return jnp.concatenate([r.tmat[blk * 128:(blk + 1) * 128, lanes], r.tmat[512 + blk * 32:512 + (blk + 1) * 32, lanes]], axis=0)
        return r.tmat[blk * B:(blk + 1) * B, lanes]

    packed = []
    for blk in range(4):
        for j in range(cols):
            put_main(blk * cols + j, rows_of(blk, slice(j * 128, (j + 1) * 128)))
        rem = rows_of(blk, slice(cols * 128, cols * 128 + 128))
        packed.append(jnp.concatenate([rem[g * RR:(g + 1) * RR] for g in range(GR)], axis=1))
    wide = jnp.dot(jnp.concatenate(packed, axis=0).astype(BF16), r.perm[:, :cols * 128], preferred_element_type=F32)
    for blk in range(4):
        for j in range(cols):
            put_rem(blk * cols + j, wide[blk * RR:(blk + 1) * RR, j * 128:(j + 1) * 128])


def update_kernel(finish, project, natural_in, *refs):
    refs = list(refs)
    take = lambda: refs.pop(0)
    r = Refs()
    r.z_in = take()
    if finish:
        t_ref = take()
        r.gin, r.bin, r.wg, r.gout, r.bout, r.wo = [take() for _ in range(6)]
    if project:
        r.perm, r.mask, r.gnext, r.bnext, r.wp = [take() for _ in range(5)]
    if finish:
        r.z_out = take()
    if project:
        t_out, r.a_in, r.b_in = [take() for _ in range(3)]
    if natural_in:
        r.z_own = take()
    if finish:
        r.y_buf, t_own, send_t, recv_t = [take() for _ in range(4)]
        if not project:
            r.zo_own = take()
    if project:
        r.sa, r.sb, r.out_a, r.out_b, r.send_sem, r.recv_sem = [take() for _ in range(6)]
        r.amat, r.bmat, r.tmat, abuf, bbuf, fetch_sem = [take() for _ in range(6)]
    step = pl.program_id(0)

    @pl.when(step == 0)
    def _():
        team = 8 if finish == 'in' else ND
        met = ND if project else team
        greet(met)
        if finish:
            pl.semaphore_wait(pltpu.get_barrier_semaphore(), met - 1)
            each, me = 128 // team, place(team)

            def give(s, grp, sem):
                there = t_own.at[pl.ds(me * each, each), s, grp]

                def send(n, inner):
                    other, device = partner(team, n)
                    pltpu.make_async_remote_copy(
                        src_ref=t_ref.at[:, other, s, grp], dst_ref=there, send_sem=send_t, recv_sem=recv_t.at[sem],
                        device_id=device, device_id_type=MESH).start()
                    return inner

                lax.fori_loop(1, team, send, 0)
                pltpu.make_async_copy(t_ref.at[:, me, s, grp], there, recv_t.at[sem]).start()

            def piece(grp, carry):
                give(0, grp, STEPS + grp)
                return carry

            def slab(s, carry):
                give(s, slice(None), s)
                return carry

            lax.fori_loop(0, 5, piece, 0)
            lax.fori_loop(1, STEPS, slab, 0)

    @pl.when(step < STEPS)
    def _():
        if finish:
            @pl.when(step > 0)
            def _():
                landed = t_own.at[:, step]
                pltpu.make_async_copy(landed, landed, recv_t.at[step]).wait()

            def arrive(grp):
                landed = t_own.at[:, 0, grp]
                pltpu.make_async_copy(landed, landed, recv_t.at[STEPS + grp]).wait()

            r.arrive = arrive
            r.tri = lambda c0, grp: t_own[c0:c0 + 16, step, grp]
        position_step(finish, project, natural_in, step, r)

    if project:
        @pl.when(step >= STEPS)
        def _():
            c = step - STEPS
            each = 16 if project == 'in' else 8
            pairs = ((r.a_in, abuf), (r.b_in, bbuf))

            def fetch(chan):
                slot = lax.rem(chan, 2)
                for k, (src, buf) in enumerate(pairs):
                    for g in range(5):
                        pltpu.make_async_copy(src.at[chan, :, g], buf.at[slot, :, pl.ds(g * RR, RR)], fetch_sem.at[k, slot]).start()

            groups = channel_groups(project)
            for q, (start, count) in enumerate(groups):
                @pl.when(c == start)
                def _():
                    for k, (src, _) in enumerate(pairs):
                        landed = group_bytes(src, q)
                        pltpu.make_async_copy(landed, landed, r.recv_sem.at[k, q]).wait()
                    fetch(c)

            slot = lax.rem(c, 2)
            for k, (_, buf) in enumerate(pairs):
                pltpu.make_async_copy(buf.at[slot], buf.at[slot], fetch_sem.at[k, slot]).wait()
            last = functools.reduce(lambda x, y: x | y, [c == start + count - 1 for start, count in groups])

            @pl.when(jnp.logical_not(last))
            def _():
                fetch(c + 1)

            r.a, r.b = abuf.at[pl.ds(slot, 1)], bbuf.at[pl.ds(slot, 1)]

            def put_main(owner, v):
                tiles = v.reshape(GR, STEPS, SL, 128).astype(BF16)
                for s in range(STEPS):
                    t_out[0, owner, s, :GR] = tiles[:, s]

            def put_rem(owner, v):
                t_out[0, owner, :, GR] = v.reshape(STEPS, SL, 128).astype(BF16)

            channel_step(project == 'in', r, put_main, put_rem)

            @pl.when(c == each - 1)
            def _():
                for k, (src, dst) in enumerate(((r.out_a, r.a_in), (r.out_b, r.b_in))):
                    if project == 'out':
                        sent = src.at[:, pl.ds(0, 128 - 8)]
                    elif k == 0:
                        sent = dst.at[pl.ds(0, 15)]
                    else:
                        sent = src.at[:, pl.ds(0, 128 - 16)]
                    pltpu.make_async_copy(sent, sent, r.send_sem.at[k]).wait()

    if finish:
        @pl.when(step == STEPS - 1)
        def _():
            team = 8 if finish == 'in' else ND
            sent = t_own.at[pl.ds(0, 128 - 128 // team)]
            pltpu.make_async_copy(sent, sent, send_t).wait()


def update_call(z, t, at, after, params, collective_id):
    kind = lambda which: None if which is None else 'in' if which[1] else 'out'
    finish, project = kind(at), kind(after)
    natural_in = z.shape[0] == GR
    slab = lambda n: jnp.minimum(n, STEPS - 1)
    z_spec = pl.BlockSpec((5, SL, 128, 128), lambda n: (0, slab(n), 0, 0))
    n_spec = pl.BlockSpec((GR, SL, B, 128), lambda n: (0, slab(n), 0, 0))
    anywhere = pl.BlockSpec(memory_space=pl.ANY)

    def weight(name, which):
        arr = params[name]
        return arr, pl.BlockSpec((1, 1) + arr.shape[2:], lambda n: tuple(which) + (0,) * (arr.ndim - 2))

    ins, outs, scratch, steps = [(z, n_spec if natural_in else z_spec)], [], [], STEPS
    if natural_in:
        scratch.append(pltpu.VMEM((5, SL, 128, 128), BF16))
    if finish:
        ins.append((t, anywhere))
        ins += [weight(name, at) for name in ('gin', 'bin', 'wg', 'gout', 'bout', 'wo')]
        outs.append((jax.ShapeDtypeStruct((5, RR, 128, 128) if project else (GR, RR, B, 128), BF16), z_spec if project else n_spec))
        scratch += [pltpu.VMEM((128 * SL, 128), F32), pltpu.VMEM((128, STEPS, 5, SL, 128), BF16)]
        scratch += [pltpu.SemaphoreType.DMA, pltpu.SemaphoreType.DMA((STEPS + 5,))]
        if not project:
            scratch.append(pltpu.VMEM((5, SL, 128, 128), BF16))
    if project:
        ins.append((params['perm'], pl.BlockSpec((512, 512), lambda n: (0, 0))))
        ins.append((params['mask'], pl.BlockSpec((5, SL, 128), lambda n: (0, slab(n), 0))))
        ins += [weight(name, after) for name in ('gin', 'bin', 'wp')]
        each, owners, width = (8, 16, 512) if project == 'out' else (16, 8, 256)
        steps += each
        outs.append((jax.ShapeDtypeStruct((each, owners, STEPS, 5, SL, 128), BF16),
                     pl.BlockSpec((1, owners, STEPS, 5, SL, 128), lambda n: (jnp.maximum(n - STEPS, 0), 0, 0, 0, 0, 0))))
        outs += [(jax.ShapeDtypeStruct((each, 4, 5, RR, w), BF16), anywhere) for w in (512, width)]
        scratch += [pltpu.VMEM((SWAP * SL, 128), F32)] * 2
        scratch += [pltpu.VMEM((STEPS, 128, 5, SL, 128), BF16)] * 2
        scratch += [pltpu.SemaphoreType.DMA((2,)), pltpu.SemaphoreType.DMA((2, len(SPLIT)))]
        scratch += [pltpu.VMEM((640, 640), BF16), pltpu.VMEM((640, width + 128), BF16), pltpu.VMEM((640, width + 128), F32)]
        scratch += [pltpu.VMEM((2, 4, 200, w), BF16) for w in (512, width)] + [pltpu.SemaphoreType.DMA((2, 2))]
    name = '_'.join((['finish', finish] if finish else []) + (['start', project] if project else []))
    return pl.pallas_call(
        functools.partial(update_kernel, finish, project, natural_in), name=name, grid=(steps,),
        in_specs=[spec for _, spec in ins], out_specs=[spec for _, spec in outs], out_shape=[shape for shape, _ in outs],
        scratch_shapes=scratch, compiler_params=pltpu.CompilerParams(
            dimension_semantics=('arbitrary',), vmem_limit_bytes=60 * 2 ** 20, collective_id=collective_id, has_side_effects=True),
    )(*[v for v, _ in ins])


def solution(mesh):
    pair_spec = P(('data', 'dap'), 'dap2', None)
    mask_spec = P(('data', 'dap'), 'dap2')

    def local_fn(pair_act, pair_mask, in_gamma, in_beta, w_proj, w_gate, out_gamma, out_beta, w_out):
        mask = to_tiles(pair_mask.astype(F32))
        z = pair_act.reshape(GR, RR, B, 128)
        src = jnp.arange(512)
        perm = (((src % 128) // 32 * 128 + src // 128 * 32 + src % 32)[:, None] == jnp.arange(512)[None, :]).astype(BF16)
        rowed = lambda v: v[:, :, None, :]
        wide = lambda v: jnp.broadcast_to(v[..., None, None], v.shape + (1, 128))
        params = dict(
            perm=perm, mask=mask, gin=rowed(in_gamma), bin=rowed(in_beta), wp=jnp.swapaxes(w_proj, 2, 3), wg=w_gate,
            gout=wide(out_gamma), bout=wide(out_beta), wo=w_out)
        layers = in_gamma.shape[0]
        t, _, _ = update_call(z, None, None, (0, 0), params, 1)
        for layer in range(layers):
            z, t, _, _ = update_call(z, t, (layer, 0), (layer, 1), params, 2 if layer == 0 else 3)
            if layer + 1 < layers:
                z, t, _, _ = update_call(z, t, (layer, 1), (layer + 1, 0), params, 4)
            else:
                z, = update_call(z, t, (layer, 1), None, params, 5)
        return z.reshape(B, B, 128)

    return jax.shard_map(local_fn, mesh=mesh, in_specs=(pair_spec, mask_spec) + (P(),) * 7, out_specs=pair_spec, check_vma=False)
```

time: 1620 us -> 1600 us (0.988)
  Pallas kernels: 1600 us -> 1570 us
    pallas_call x7 -> x5, Pallas kernels: 1600 us -> 1570 us  [update_call(): pl.pallas_call(functools.partial(update_kernel, finish, project, natural_...]
where the time goes in v4:
time: 1600 us; the launch traced here: 1590 us
  Pallas kernels  1570 us (98%)
    pallas_call x5, Pallas kernels, update_call(): pl.pallas_call(functools.partial(update_kernel, finish, project, natural_...  1570 us

profile of v4, /device:TPU:0, one launch (start us, length us, event | category | flops | bytes accessed | tf_op | source)
XLA Modules:
  0.0 1590.5 jit_solution(3396963419889585998)
XLA Ops:
  0.0 0.9 convert_element_type.13
  1.0 0.1 reshape.66
  1.1 0.6 pad_maximum_fusion.refs_2_.refs_9_
  1.8 2.0 broadcast_in_dim.10.refs_5_
  3.7 2.0 broadcast_in_dim.11.refs_6_
  5.7 0.9 fusion.refs_1_.refs_8_
  6.7 2.0 copy.13
  8.7 296.8 %start_out.1 = (bf16[8,16,5,5,8,128]{5,4,3,2,1,0:T(8,128)(2,1)}, bf16[8,4,5,40,512]{4,3,2,1,0:T(8,128)(2,1)}, bf16[8,4,5,40,512]{4,3,2,1,0:T(8,128)(2,1)}) custom-call(bf16[4,40,160,128]{3,2,1,0:T(8,128)(2,1)} %bitcast.8, bf16[512,512]{1,0:T(8,128)(2,1)} %fusion.refs_1_.refs_8_, f32[5,40,128]{2,1,0:T(8,128)} %pad_maximum_fusion.refs_2_.refs_9_, ...), custom_call_target="tpu_custom_call" | custom-call | tf_op jit(solution)/shard_map/start_out/pallas_call | solution.py:443
  305.5 433.6 %finish_out_start_in.2 = (bf16[5,40,128,128]{3,2,1,0:T(8,128)(2,1)}, bf16[16,8,5,5,8,128]{5,4,3,2,1,0:T(8,128)(2,1)}, bf16[16,4,5,40,512]{4,3,2,1,0:T(8,128)(2,1)}, bf16[16,4,5,40,256]{4,3,2,1,0:T(8,128)(2,1)}) custom-call(bf16[4,40,160,128]{3,2,1,0:T(8,128)(2,1)} %bitcast.9, bf16[8,16,5,5,8,128]{5,4,3,2,1,0:T(8,128)(2,1)} %get-tuple-element.12.refs_1_, ...), custom_call_target="tpu_custom_call" | custom-call | tf_op jit(solution)/shard_map/finish_out_start_in/pallas_call | solution.py:443
  739.1 325.9 %finish_in_start_out.1 = (bf16[5,40,128,128]{3,2,1,0:T(8,128)(2,1)}, bf16[8,16,5,5,8,128]{5,4,3,2,1,0:T(8,128)(2,1)}, bf16[8,4,5,40,512]{4,3,2,1,0:T(8,128)(2,1)}, bf16[8,4,5,40,512]{4,3,2,1,0:T(8,128)(2,1)}) custom-call(bf16[5,40,128,128]{3,2,1,0:T(8,128)(2,1)} %get-tuple-element.13.refs_0_, bf16[16,8,5,5,8,128]{5,4,3,2,1,0:T(8,128)(2,1)} %get-tuple-element.14.refs_1_, ...), custom_call_target="tpu_custom_call" | custom-call | tf_op jit(solution)/shard_map/finish_in_start_out/pallas_call | solution.py:443
  1065.0 434.0 %finish_out_start_in.3 = (bf16[5,40,128,128]{3,2,1,0:T(8,128)(2,1)}, bf16[16,8,5,5,8,128]{5,4,3,2,1,0:T(8,128)(2,1)}, bf16[16,4,5,40,512]{4,3,2,1,0:T(8,128)(2,1)}, bf16[16,4,5,40,256]{4,3,2,1,0:T(8,128)(2,1)}) custom-call(bf16[5,40,128,128]{3,2,1,0:T(8,128)(2,1)} %get-tuple-element.15.refs_0_, bf16[8,16,5,5,8,128]{5,4,3,2,1,0:T(8,128)(2,1)} %get-tuple-element.16.refs_1_, ...), custom_call_target="tpu_custom_call" | custom-call | tf_op jit(solution)/shard_map/finish_out_start_in/pallas_call | solution.py:443
  1499.0 84.7 %finish_in.1 = bf16[4,40,160,128]{3,2,1,0:T(8,128)(2,1)} custom-call(bf16[5,40,128,128]{3,2,1,0:T(8,128)(2,1)} %get-tuple-element.17.refs_0_, bf16[16,8,5,5,8,128]{5,4,3,2,1,0:T(8,128)(2,1)} %get-tuple-element.18.refs_1_, f32[2,2,1,128]{3,2,1,0:T(1,128)} %bitcast.24, f32[2,2,1,128]{3,2,1,0:T(1,128)} %bitcast.32, bf16[2,2,128,128]{3,2,1,0:T(8,128)(2,1)} %refs_4_.7, ...), custom_call_target="tpu_custom_call" | custom-call | tf_op jit(solution)/shard_map/finish_in/pallas_call | solution.py:443
  1583.7 6.8 copy.15
  (4 shorter events, 0.0 us)

commit v5 on v4

--- a/solution.py
+++ b/solution.py
@@ -17,7 +17,8 @@
 RR = 40
 SL = 8
 STEPS = RR // SL
-UNROLL = 4
+UNROLL = 8
+LEAD = 2
 SPLIT = (2, 4, 8, 8)
 SWAP = 136
 
@@ -145,7 +146,7 @@
             scale = lax.rsqrt(total * (1.0 / 128) + NORM_EPS)[None]
             for cb in range(8):
                 sl = slice(cb * 16, (cb + 1) * 16)
-                y = (r.tri(cb * 16, grp).astype(F32) - mean) * scale * r.gout[0, 0, sl] + r.bout[0, 0, sl]
+                y = (r.tri(cb * 16, grp).astype(F32) - mean) * scale * r.gout[0, 0, sl][:, None] + r.bout[0, 0, sl][:, None]
                 r.y_buf[cb * 128:(cb + 1) * 128, :] = y.reshape(128, 128)
 
         def tile(n, inner):
@@ -290,27 +291,28 @@
         r.amat, r.bmat, r.tmat, abuf, bbuf, fetch_sem = [take() for _ in range(6)]
     step = pl.program_id(0)
 
+    team = 8 if finish == 'in' else ND
+    each, me = 128 // team, place(team)
+
+    def give(s, grp, sem):
+        there = t_own.at[pl.ds(me * each, each), s, grp]
+
+        def send(n, inner):
+            other, device = partner(team, n)
+            pltpu.make_async_remote_copy(
+                src_ref=t_ref.at[:, other, s, grp], dst_ref=there, send_sem=send_t, recv_sem=recv_t.at[sem],
+                device_id=device, device_id_type=MESH).start()
+            return inner
+
+        lax.fori_loop(1, team, send, 0)
+        pltpu.make_async_copy(t_ref.at[:, me, s, grp], there, recv_t.at[sem]).start()
+
     @pl.when(step == 0)
     def _():
-        team = 8 if finish == 'in' else ND
         met = ND if project else team
         greet(met)
         if finish:
             pl.semaphore_wait(pltpu.get_barrier_semaphore(), met - 1)
-            each, me = 128 // team, place(team)
-
-            def give(s, grp, sem):
-                there = t_own.at[pl.ds(me * each, each), s, grp]
-
-                def send(n, inner):
-                    other, device = partner(team, n)
-                    pltpu.make_async_remote_copy(
-                        src_ref=t_ref.at[:, other, s, grp], dst_ref=there, send_sem=send_t, recv_sem=recv_t.at[sem],
-                        device_id=device, device_id_type=MESH).start()
-                    return inner
-
-                lax.fori_loop(1, team, send, 0)
-                pltpu.make_async_copy(t_ref.at[:, me, s, grp], there, recv_t.at[sem]).start()
 
             def piece(grp, carry):
                 give(0, grp, STEPS + grp)
@@ -321,7 +323,7 @@
                 return carry
 
             lax.fori_loop(0, 5, piece, 0)
-            lax.fori_loop(1, STEPS, slab, 0)
+            lax.fori_loop(1, LEAD if project else STEPS, slab, 0)
 
     @pl.when(step < STEPS)
     def _():
@@ -338,6 +340,10 @@
             r.arrive = arrive
             r.tri = lambda c0, grp: t_own[c0:c0 + 16, step, grp]
         position_step(finish, project, natural_in, step, r)
+        if finish and project:
+            @pl.when(step + LEAD < STEPS)
+            def _():
+                give(step + LEAD, slice(None), step + LEAD)
 
     if project:
         @pl.when(step >= STEPS)
@@ -458,7 +464,7 @@
         src = jnp.arange(512)
         perm = (((src % 128) // 32 * 128 + src // 128 * 32 + src % 32)[:, None] == jnp.arange(512)[None, :]).astype(BF16)
         rowed = lambda v: v[:, :, None, :]
-        wide = lambda v: jnp.broadcast_to(v[..., None, None], v.shape + (1, 128))
+        wide = lambda v: jnp.broadcast_to(v[..., None], v.shape + (128,))
         params = dict(
             perm=perm, mask=mask, gin=rowed(in_gamma), bin=rowed(in_beta), wp=jnp.swapaxes(w_proj, 2, 3), wg=w_gate,
             gout=wide(out_gamma), bout=wide(out_beta), wo=w_out)

time: 1600 us -> 1590 us (level)
  no operation moved by 1% of the time
where the time goes in v5:
time: 1590 us; the launch traced here: 1580 us
  Pallas kernels  1570 us (99%)
    pallas_call x5, Pallas kernels, update_call(): pl.pallas_call(functools.partial(update_kernel, finish, project, natural_...  1570 us

profile of v5, /device:TPU:0, one launch (start us, length us, event | category | flops | bytes accessed | tf_op | source)
XLA Modules:
  0.0 1581.7 jit_solution(11597859506589440655)
XLA Ops:
  0.0 0.9 convert_element_type.13
  1.0 0.1 reshape.62
  1.1 0.6 pad_maximum_fusion.refs_2_.refs_9_
  1.8 1.5 broadcast_in_dim.10.refs_5_
  3.3 1.5 broadcast_in_dim.11.refs_6_
  4.8 0.9 fusion.refs_1_.refs_8_
  5.7 2.0 copy.13
  7.8 295.1 %start_out.1 = (bf16[8,16,5,5,8,128]{5,4,3,2,1,0:T(8,128)(2,1)}, bf16[8,4,5,40,512]{4,3,2,1,0:T(8,128)(2,1)}, bf16[8,4,5,40,512]{4,3,2,1,0:T(8,128)(2,1)}) custom-call(bf16[4,40,160,128]{3,2,1,0:T(8,128)(2,1)} %bitcast.8, bf16[512,512]{1,0:T(8,128)(2,1)} %fusion.refs_1_.refs_8_, f32[5,40,128]{2,1,0:T(8,128)} %pad_maximum_fusion.refs_2_.refs_9_, ...), custom_call_target="tpu_custom_call" | custom-call | tf_op jit(solution)/shard_map/start_out/pallas_call | solution.py:449
  302.9 438.5 %finish_out_start_in.2 = (bf16[5,40,128,128]{3,2,1,0:T(8,128)(2,1)}, bf16[16,8,5,5,8,128]{5,4,3,2,1,0:T(8,128)(2,1)}, bf16[16,4,5,40,512]{4,3,2,1,0:T(8,128)(2,1)}, bf16[16,4,5,40,256]{4,3,2,1,0:T(8,128)(2,1)}) custom-call(bf16[4,40,160,128]{3,2,1,0:T(8,128)(2,1)} %bitcast.9, bf16[8,16,5,5,8,128]{5,4,3,2,1,0:T(8,128)(2,1)} %get-tuple-element.12.refs_1_, ...), custom_call_target="tpu_custom_call" | custom-call | tf_op jit(solution)/shard_map/finish_out_start_in/pallas_call | solution.py:449
  741.5 316.4 %finish_in_start_out.1 = (bf16[5,40,128,128]{3,2,1,0:T(8,128)(2,1)}, bf16[8,16,5,5,8,128]{5,4,3,2,1,0:T(8,128)(2,1)}, bf16[8,4,5,40,512]{4,3,2,1,0:T(8,128)(2,1)}, bf16[8,4,5,40,512]{4,3,2,1,0:T(8,128)(2,1)}) custom-call(bf16[5,40,128,128]{3,2,1,0:T(8,128)(2,1)} %get-tuple-element.13.refs_0_, bf16[16,8,5,5,8,128]{5,4,3,2,1,0:T(8,128)(2,1)} %get-tuple-element.14.refs_1_, ...), custom_call_target="tpu_custom_call" | custom-call | tf_op jit(solution)/shard_map/finish_in_start_out/pallas_call | solution.py:449
  1057.9 434.5 %finish_out_start_in.3 = (bf16[5,40,128,128]{3,2,1,0:T(8,128)(2,1)}, bf16[16,8,5,5,8,128]{5,4,3,2,1,0:T(8,128)(2,1)}, bf16[16,4,5,40,512]{4,3,2,1,0:T(8,128)(2,1)}, bf16[16,4,5,40,256]{4,3,2,1,0:T(8,128)(2,1)}) custom-call(bf16[5,40,128,128]{3,2,1,0:T(8,128)(2,1)} %get-tuple-element.15.refs_0_, bf16[8,16,5,5,8,128]{5,4,3,2,1,0:T(8,128)(2,1)} %get-tuple-element.16.refs_1_, ...), custom_call_target="tpu_custom_call" | custom-call | tf_op jit(solution)/shard_map/finish_out_start_in/pallas_call | solution.py:449
  1492.4 82.5 %finish_in.1 = bf16[4,40,160,128]{3,2,1,0:T(8,128)(2,1)} custom-call(bf16[5,40,128,128]{3,2,1,0:T(8,128)(2,1)} %get-tuple-element.17.refs_0_, bf16[16,8,5,5,8,128]{5,4,3,2,1,0:T(8,128)(2,1)} %get-tuple-element.18.refs_1_, f32[2,2,1,128]{3,2,1,0:T(1,128)} %bitcast.24, f32[2,2,1,128]{3,2,1,0:T(1,128)} %bitcast.32, bf16[2,2,128,128]{3,2,1,0:T(8,128)(2,1)} %refs_4_.7, ...), custom_call_target="tpu_custom_call" | custom-call | tf_op jit(solution)/shard_map/finish_in/pallas_call | solution.py:449
  1574.9 6.8 copy.15
  (4 shorter events, 0.0 us)
